TPU v7x, 8 devices: a whole 2x2x1 slice. The times are simulated.
8 devices in a mesh: data: 1 (over z), tp: 2 (over y), ep: 4 (over x, core).
Axes of the slice: x: 2, y: 2, z: 1, core: 2. Of those that a mesh axis runs over, the one named last changes fastest.
Arguments:
- tokens: bfloat16 [1024, 1280], P(('data', 'ep', 'tp'))
- expert_ids: int32 [1024, 6], P(('data', 'ep', 'tp'))
- gate_vals: float32 [1024, 6], P(('data', 'ep', 'tp'))
- slot_ids: int32 [1024, 6], P(('data', 'ep', 'tp'))
- send_counts: int32 [8, 64], P(('data', 'ep', 'tp'))
- shared_w1: bfloat16 [1280, 1792], P(None, 'tp')
- shared_w3: bfloat16 [1280, 1792], P(None, 'tp')
- shared_w2: bfloat16 [1792, 1280], P('tp')
- expert_w1: bfloat16 [64, 1280, 896], P('ep')
- expert_w3: bfloat16 [64, 1280, 896], P('ep')
- expert_w2: bfloat16 [64, 896, 1280], P('ep')
Outputs:
- output: bfloat16 [1024, 1280], P(('data', 'ep', 'tp'))
All inputs are finite; a program needn't handle non-finite values.
Results may differ from a plain program's by a relative error of at most 0.00104.
Values are sent between devices in bfloat16 or wider.
A program may use at most 1 GiB of HBM per device.

v0:
```python
import jax
import jax.numpy as jnp
from jax import lax
from jax.sharding import PartitionSpec as P

CAP_FACTOR = 4


def capacity_rows(n_tok, top_k, n_exp):
    return min(n_tok, ((CAP_FACTOR * n_tok * top_k // n_exp + 7) // 8) * 8)


def solution(mesh):
    ep_size = mesh.shape["ep"]
    row_spec = P(("data", "ep", "tp"), None)
    expert_spec = P("ep", None, None)

    def layer_body(tokens, expert_ids, gate_vals, slot_ids, send_counts, shared_w1, shared_w3, shared_w2, expert_w1, expert_w3, expert_w2):
        n_tok, d_model = tokens.shape
        top_k = expert_ids.shape[1]
        n_local = expert_w1.shape[0]
        n_exp = n_local * ep_size
        capacity = capacity_rows(n_tok, top_k, n_exp)
        n_rows = n_exp * capacity

        gathered = lax.all_gather(tokens, "tp", axis=0, tiled=True)
        pre_gate = jnp.dot(gathered, shared_w1, preferred_element_type=jnp.float32)
        pre_up = jnp.dot(gathered, shared_w3, preferred_element_type=jnp.float32)
        shared_hidden = (jax.nn.silu(pre_gate) * pre_up).astype(jnp.bfloat16)
        part_sum = jnp.dot(shared_hidden, shared_w2, preferred_element_type=jnp.float32)
        shared_out = lax.psum_scatter(part_sum, "tp", scatter_dimension=0, tiled=True)

        row_limit = jnp.take(send_counts[0], expert_ids, axis=0)
        kept_mask = (slot_ids >= 0) & (slot_ids < row_limit)
        dest_row = jnp.where(kept_mask, expert_ids * capacity + slot_ids, n_rows)
        tok_ids = jnp.broadcast_to(jnp.arange(n_tok, dtype=jnp.int32)[:, None], (n_tok, top_k)).reshape(-1)
        owner_ids = jnp.full((n_rows,), n_tok, jnp.int32).at[dest_row.reshape(-1)].set(tok_ids, mode="drop")
        send_buf = jnp.take(tokens, owner_ids, axis=0, mode="fill", fill_value=0)
        send_buf = send_buf.reshape(ep_size, n_local, capacity, d_model)
        recv_buf = lax.all_to_all(send_buf, "ep", 0, 2, tiled=True)
        recv_buf = recv_buf.reshape(n_local, ep_size * capacity, d_model)

        exp_gate = jnp.einsum("erd,edf->erf", recv_buf, expert_w1, preferred_element_type=jnp.float32)
        exp_up = jnp.einsum("erd,edf->erf", recv_buf, expert_w3, preferred_element_type=jnp.float32)
        exp_hidden = (jax.nn.silu(exp_gate) * exp_up).astype(jnp.bfloat16)
        exp_out = jnp.einsum("erf,efd->erd", exp_hidden, expert_w2, preferred_element_type=jnp.float32).astype(jnp.bfloat16)
        back_buf = lax.all_to_all(exp_out.reshape(1, n_local, ep_size * capacity, d_model), "ep", 2, 0, tiled=True)

        back_rows = back_buf.reshape(n_rows, d_model)
        picked = jnp.take(back_rows, dest_row, axis=0, mode="fill", fill_value=0)
        gate_eff = jnp.where(kept_mask, gate_vals, 0.0)
        routed_sum = jnp.sum(gate_eff[:, :, None] * picked.astype(jnp.float32), axis=1)
        return (tokens.astype(jnp.float32) + shared_out + routed_sum).astype(jnp.bfloat16)

    return jax.shard_map(
        layer_body,
        mesh=mesh,
        in_specs=(row_spec, row_spec, row_spec, row_spec, row_spec, P(None, "tp"), P(None, "tp"), P("tp", None), expert_spec, expert_spec, expert_spec),
        out_specs=row_spec,
        check_vma=False,
    )
```

profile of v0, /device:TPU:0, one launch (start us, length us, event | category | flops | bytes accessed | tf_op | source)
XLA Modules:
  0.0 331.5 jit_solution(18183389337754553244)
XLA Ops:
  6.5 0.0 copy-start
  6.5 0.0 copy-start.1
  6.5 0.9 compare_select_fusion.3
  7.4 0.1 copy.46
  7.5 0.1 reshape.75
  7.7 0.0 copy-done.1
  7.7 0.0 copy-start.3
  7.7 0.0 copy-start.5
  7.7 4.8 %gather_fusion = s32[768]{0:T(1024)S(1)} fusion(s32[64]{0:T(128)S(1)} %bitcast.22, s32[1024]{0:T(1024)S(1)} %pad_clamp_fusion.1), kind=kCustom, calls=%fused_computation | custom fusion | bytes 9216 | tf_op jit(solution)/shard_map/jit(_take)/gather | solution.py:33
  12.5 0.0 copy-start.2
  12.5 0.1 reshape.74
  12.6 0.1 copy.47
  12.7 0.0 copy-done.3
  12.7 0.0 copy-done.5
  12.7 0.1 copy.50
  12.9 0.1 reshape.68
  13.0 0.1 reshape.101
  13.2 3.4 %scatter_custom_fusion = s32[3072]{0:T(1024)S(1)} fusion(s32[768]{0:T(1024)S(1)} %fusion.15, s32[768]{0:T(1024)S(1)} %reshape.101, s32[]{:T(128)} %constant.56.clone.1), kind=kCustom, calls=%fused_computation.26 | custom fusion | bytes 12292 | tf_op jit(solution)/shard_map/scatter | solution.py:37
  16.6 0.1 broadcast_in_dim.60
  16.7 0.0 copy-done.2
  16.7 14.3 %gather_fusion.1 = bf16[3072,1280]{1,0:T(8,128)(2,1)} fusion(bf16[128,1280]{1,0:T(8,128)(2,1)S(1)} %copy-done.2, s32[3072]{0:T(1024)S(1)} %fusion.11), kind=kCustom, calls=%fused_computation.1 | custom fusion | bytes 15740928 | tf_op jit(solution)/shard_map/jit(_take)/gather | solution.py:38
  31.0 4.2 %broadcast_select_fusion = bf16[4,16,48,1280]{3,2,1,0:T(8,128)(2,1)S(1)} fusion(bf16[4,16,48,1280]{3,2,1,0:T(8,128)(2,1)} %bitcast.26, pred[4,16,48]{2,1,0:T(8,128)(4,1)S(1)} %broadcast_in_dim.60), kind=kLoop, calls=%fused_computation.6 | loop fusion | flops 3932160 | bytes 15731712 | tf_op jit(solution)/shard_map/jit(_take)/select_n | solution.py:38
  35.2 92.3 %all_to_all.30 = bf16[4,16,48,1280]{3,2,1,0:T(8,128)(2,1)} all-to-all(bf16[4,16,48,1280]{3,2,1,0:T(8,128)(2,1)S(1)} %broadcast_select_fusion), channel_id=1, replica_groups=mesh['data'=1,'tp'=2,'ep'=4] {'ep'}, dimensions={0} | all-to-all | bytes 15728640 | tf_op jit(solution)/shard_map/all_to_all | solution.py:40
  127.6 7.2 %copy.51 = bf16[1,16,4,48,1280]{4,3,2,1,0:T(8,128)(2,1)} copy(bf16[1,16,4,48,1280]{4,3,1,2,0:T(8,128)(2,1)} %bitcast.27) | data formatting | bytes 15728640 | tf_op jit(solution)/shard_map/all_to_all | solution.py:40
  134.8 22.5 %fusion.20 = f32[16,192,896]{2,1,0:T(8,128)} fusion(bf16[16,192,1280]{2,1,0:T(8,128)(2,1)} %bitcast.24, bf16[16,1280,896]{2,1,0:T(8,128)(2,1)} %param.19), kind=kOutput, calls=%fused_computation.39 | convolution fusion | flops 7046430720 | bytes 55574528 | tf_op jit(solution)/shard_map/erd,edf->erf/dot_general | solution.py:43
  157.3 35.3 %convert_bitcast_fusion = bf16[1,16,192,1280]{3,2,1,0:T(8,128)(2,1)} fusion(bf16[16,896,1280]{2,1,0:T(8,128)(2,1)} %param.21, f32[16,192,896]{2,1,0:T(8,128)} %fusion.20, bf16[16,192,1280]{2,1,0:T(8,128)(2,1)} %bitcast.25, bf16[16,1280,896]{2,1,0:T(8,128)(2,1)} %param.20), kind=kOutput, calls=%fused_computation.5 | convolution fusion | flops 14113308672 | bytes 100139008 | tf_op jit(solution)/shard_map/erf,efd->erd/dot_general | solution.py:46
  192.5 10.8 %copy.52 = bf16[1,16,192,1280]{3,1,0,2:T(8,128)(2,1)} copy(bf16[1,16,192,1280]{3,2,1,0:T(8,128)(2,1)} %convert_bitcast_fusion) | data formatting | bytes 15728640 | tf_op jit(solution)/shard_map/reshape | solution.py:47
  203.3 5.5 %all-to-all-start.1 = ((bf16[1,16,192,1280]{3,1,0,2:T(8,128)(2,1)}), bf16[1,16,192,1280]{3,1,0,2:T(8,128)(2,1)}, u32[]{:S(2)}, u32[]{:S(2)}) async-start(bf16[1,16,192,1280]{3,1,0,2:T(8,128)(2,1)} %copy.52), calls=%async_computation.2 | async-start | bytes 15728640 | tf_op jit(solution)/shard_map/all_to_all | solution.py:47
  208.8 0.3 reduce-scatter.2.cloned.1.call-start
  209.1 10.9 %all_gather.3 = bf16[256,1280]{1,0:T(8,128)(2,1)S(1)} all-gather(bf16[128,1280]{1,0:T(8,128)(2,1)S(1)} %copy-done.2), channel_id=1, replica_groups=mesh['data'=1,'tp'=2,'ep'=4] {'tp'}, dimensions={0}, use_global_device_ids=true | all-gather | bytes 983040 | tf_op jit(solution)/shard_map/all_gather | solution.py:26
  220.0 0.0 copy-start.4
  220.0 3.4 %fusion.19 = f32[256,896]{1,0:T(8,128)} fusion(bf16[256,1280]{1,0:T(8,128)(2,1)S(1)} %all_gather.3, bf16[1280,896]{1,0:T(8,128)(2,1)} %param.16), kind=kOutput, calls=%fused_computation.38 | convolution fusion | flops 587202560 | bytes 3866624 | tf_op jit(solution)/shard_map/dot_general | solution.py:27
  223.4 0.0 copy-done
  223.4 4.6 %fusion.4 = f32[256,1280]{1,0:T(8,128)} fusion(bf16[896,1280]{1,0:T(8,128)(2,1)S(1)} %copy-done, bf16[256,1280]{1,0:T(8,128)(2,1)S(1)} %all_gather.3, bf16[1280,896]{1,0:T(8,128)(2,1)} %param.17, f32[256,896]{1,0:T(8,128)} %fusion.19), kind=kOutput, calls=%fused_computation.12 | convolution fusion | flops 1175781376 | bytes 7471104 | tf_op jit(solution)/shard_map/dot_general | solution.py:30
  228.0 0.0 reduce-scatter.2.cloned.1.call-update
  228.0 0.1 copy.54
  228.2 0.1 reshape.91
  228.3 0.0 copy-done.4
  228.3 0.1 copy.48
  228.4 0.1 copy.49
  228.6 67.5 %all-to-all-done.1 = bf16[1,16,192,1280]{3,1,0,2:T(8,128)(2,1)} async-done(((bf16[1,16,192,1280]{3,1,0,2:T(8,128)(2,1)}), bf16[1,16,192,1280]{3,1,0,2:T(8,128)(2,1)}, u32[]{:S(2)}, u32[]{:S(2)}) %all-to-all-start.1) | async-done | bytes 7864352 | tf_op jit(solution)/shard_map/all_to_all | solution.py:47
  296.0 9.2 %copy.53 = bf16[1,16,4,48,1280]{4,3,1,2,0:T(8,128)(2,1)} copy(bf16[1,16,4,48,1280]{4,1,3,2,0:T(8,128)(2,1)} %bitcast.6) | data formatting | bytes 15728640 | tf_op jit(solution)/shard_map/all_to_all | solution.py:47
  305.2 9.4 %gather_fusion.2 = bf16[768,1280]{1,0:T(8,128)(2,1)} fusion(bf16[3072,1280]{1,0:T(8,128)(2,1)} %bitcast.23, s32[1024]{0:T(1024)S(1)} %pad_clamp_fusion), kind=kCustom, calls=%fused_computation.2 | custom fusion | bytes 3935232 | tf_op jit(solution)/shard_map/jit(_take)/gather | solution.py:50
  314.7 4.1 %reshape.90 = bf16[128,6,1280]{2,1,0:T(8,128)(2,1)} reshape(bf16[768,1280]{1,0:T(8,128)(2,1)} %gather_fusion.2) | data formatting | bytes 3932160 | tf_op jit(solution)/shard_map/jit(_take)/gather | solution.py:50
  318.8 4.0 %multiply_reduce_fusion = f32[128,1280]{1,0:T(8,128)S(1)} fusion(bf16[128,6,1280]{2,1,0:T(8,128)(2,1)} %reshape.90, f32[128,6]{1,0:T(8,128)S(1)} %copy.48, pred[128,6]{1,0:T(8,128)(4,1)S(1)} %copy.49), kind=kLoop, calls=%fused_computation.9 | loop fusion | flops 3768320 | bytes 2625280 | tf_op jit(solution)/shard_map/reduce_sum | solution.py:52
  322.8 0.0 reduce-scatter.2.cloned.1.call-done
  322.8 1.9 add_convert_fusion
  (9 shorter events, 0.1 us)
Async XLA Ops:
  6.5 216.9 %copy-start = (bf16[896,1280]{1,0:T(8,128)(2,1)S(1)}, bf16[896,1280]{1,0:T(8,128)(2,1)}, u32[]{:S(2)}) copy-start(bf16[896,1280]{1,0:T(8,128)(2,1)} %param.18) | copy-start | bytes 6881284
  6.5 1.1 copy-start.1
  7.7 5.0 %copy-start.3 = (s32[128,6]{0,1:T(8,128)S(1)}, s32[128,6]{0,1:T(8,128)}, u32[]{:S(2)}) copy-start(s32[128,6]{0,1:T(8,128)} %param.12) | copy-start | bytes 9220
  7.7 5.0 %copy-start.5 = (s32[128,6]{0,1:T(8,128)S(1)}, s32[128,6]{0,1:T(8,128)}, u32[]{:S(2)}) copy-start(s32[128,6]{0,1:T(8,128)} %param.14) | copy-start | bytes 9220
  12.5 4.2 %copy-start.2 = (bf16[128,1280]{1,0:T(8,128)(2,1)S(1)}, bf16[128,1280]{1,0:T(8,128)(2,1)}, u32[]{:S(2)}) copy-start(bf16[128,1280]{1,0:T(8,128)(2,1)} %param.11) | copy-start | bytes 983044
  203.3 92.7 %all-to-all-start.1 = ((bf16[1,16,192,1280]{3,1,0,2:T(8,128)(2,1)}), bf16[1,16,192,1280]{3,1,0,2:T(8,128)(2,1)}, u32[]{:S(2)}, u32[]{:S(2)}) async-start(bf16[1,16,192,1280]{3,1,0,2:T(8,128)(2,1)} %copy.52), calls=%async_computation.2 | async-start | bytes 15728640 | tf_op jit(solution)/shard_map/all_to_all | solution.py:47
  208.8 113.9 %reduce-scatter.2.cloned.1.call-start = ((), (), s32[]{:S(2)}) async-start(), calls=%async_computation.3 | async-start | bytes 1966080 | tf_op jit(solution)/shard_map/reduce_scatter | solution.py:31
  220.0 8.3 %copy-start.4 = (f32[128,6]{0,1:T(8,128)S(1)}, f32[128,6]{0,1:T(8,128)}, u32[]{:S(2)}) copy-start(f32[128,6]{0,1:T(8,128)} %param.13) | copy-start | bytes 9220
Sparse Core Ops, SparseCore 0:
  228.1 21.7 reduce-scatter.1
where the time goes:
time: 332 us
  blocking collectives  103 us (31%)
  waiting for transfers between devices  67.5 us (20%)
  matrix products  65.7 us (20%)
  local copies, waits for them, and re-layouts  64.6 us (19%)
  between operations  13.6 us (4%)
  other arithmetic  11.1 us (3%)
  starting transfers between devices  5.8 us (2%)
    all_to_all x1, blocking collectives, layer_body(): recv_buf = lax.all_to_all(send_buf, 'ep', 0, 2, tiled=True)  92.3 us
    all_to_all x1, waiting for transfers between devices, layer_body(): lax.all_to_all(exp_out.reshape(1, n_local, ep_size * capacity, d_model),...  67.5 us
    dot_general x1, matrix products, layer_body(): jnp.einsum('erf,efd->erd', exp_hidden, expert_w2, preferred_element_type=...  35.3 us
    dot_general x1, matrix products, layer_body(): jnp.einsum('erd,edf->erf', recv_buf, expert_w1, preferred_element_type=jn...  22.5 us
    gather x1, local copies, waits for them, and re-layouts, layer_body(): send_buf = jnp.take(tokens, owner_ids, axis=0, mode='fill', fill_value=0)  14.3 us
    gather x2, local copies, waits for them, and re-layouts, layer_body(): picked = jnp.take(back_rows, dest_row, axis=0, mode='fill', fill_value=0)  13.5 us
    all_gather x1, blocking collectives, layer_body(): gathered = lax.all_gather(tokens, 'tp', axis=0, tiled=True)  10.9 us
    reshape x1, local copies, waits for them, and re-layouts, layer_body(): exp_out.reshape(1, n_local, ep_size * capacity, d_model)  10.8 us
  transfers between devices with their start and end apart: 2, of which 1 were waited for; matrix products, arithmetic and copies ran while one was open for 11% of the time, Pallas kernels for 0%

commit v1 on v0

v1 whole, which is shorter than its diff:
```python
import functools

import jax
import jax.numpy as jnp
from jax import lax
from jax.experimental import pallas as pl
from jax.experimental.pallas import tpu as pltpu
from jax.sharding import PartitionSpec as P

CAP_FACTOR = 4
BF16_MAX = 3.3895313892515355e38
SLOTS = 6

X_PART, X_FAR, X_Y, X_RELAY, M_PART, M_FAR, M_RELAY, S_Y, A_PART, B_FAR, C_PART = range(11)
N_COPIES = 11


def capacity_rows(n_tok, top_k, n_exp):
    return min(n_tok, ((CAP_FACTOR * n_tok * top_k // n_exp + 7) // 8) * 8)


def chunks(n, step=256):
    return [(i, min(step, n - i)) for i in range(0, n, step)]


def dot(a, b):
    return jnp.dot(a, b, preferred_element_type=jnp.float32)


def dot_nt(a, b):
    return lax.dot_general(a, b, (((1,), (1,)), ((), ())), preferred_element_type=jnp.float32)


def kernel(cap, n_local, n_exp,
           x_hbm, idx_hbm, gate_hbm, slot_hbm, cnt_hbm,
           ws1_hbm, ws3_hbm, ws2_hbm, w1_hbm, w3_hbm, w2_hbm,
           y_ref,
           xs, xy, idx_v, gate_v, slot_v, cnt_v, ms, w13b, w2b, xr, hf, hb, gm,
           s_own, s_send, s_recv, a_send, a_recv, b_send, b_recv, c_send, c_recv,
           in_sem, w_sem, send_sem, recv_sem):
    n_tok, d_model = x_hbm.shape
    top_k = idx_hbm.shape[1]
    ff = w1_hbm.shape[2]
    n_rows = n_local * cap

    ep = lax.axis_index("ep")
    tp = lax.axis_index("tp")
    part = ep + 1 - 2 * lax.rem(ep, 2)
    far = lax.rem(ep + 2, 4)
    far_part = lax.rem(part + 2, 4)

    x_in = pltpu.make_async_copy(x_hbm, xs.at[ep], in_sem.at[0])
    small = [
        pltpu.make_async_copy(idx_hbm, idx_v, in_sem.at[1]),
        pltpu.make_async_copy(gate_hbm, gate_v, in_sem.at[2]),
        pltpu.make_async_copy(slot_hbm, slot_v, in_sem.at[3]),
        pltpu.make_async_copy(cnt_hbm, cnt_v, in_sem.at[4]),
    ]
    x_in.start()
    for cp in small:
        cp.start()

    def weight_copies(r1, r3, r2, slot):
        return [
            pltpu.make_async_copy(r1, w13b.at[slot, :, pl.ds(0, ff)], w_sem.at[slot, 0]),
            pltpu.make_async_copy(r3, w13b.at[slot, :, pl.ds(ff, ff)], w_sem.at[slot, 1]),
            pltpu.make_async_copy(r2, w2b.at[slot], w_sem.at[slot, 2]),
        ]

    def expert_copies(e, slot):
        return weight_copies(w1_hbm.at[e], w3_hbm.at[e], w2_hbm.at[e], slot)

    shared_copies = weight_copies(ws1_hbm, ws3_hbm, ws2_hbm, 0)
    for cp in shared_copies:
        cp.start()
    for e in range(SLOTS - 1):
        for cp in expert_copies(e, e + 1):
            cp.start()

    barrier = pltpu.get_barrier_semaphore()
    for dev in ({"ep": part}, {"ep": far}, {"tp": 1 - tp}):
        pl.semaphore_signal(barrier, inc=1, device_id=dev, device_id_type=pl.DeviceIdType.MESH)
    pl.semaphore_wait(barrier, 3)

    def remote(src, dst, k, dev):
        return pltpu.make_async_remote_copy(
            src_ref=src, dst_ref=dst, send_sem=send_sem.at[k], recv_sem=recv_sem.at[k],
            device_id=dev, device_id_type=pl.DeviceIdType.MESH)

    x_in.wait()
    x_far = remote(xs.at[ep], xs.at[ep], X_FAR, {"ep": far})
    x_y = remote(xs.at[ep], xy, X_Y, {"tp": 1 - tp})
    x_part = remote(xs.at[ep], xs.at[ep], X_PART, {"ep": part})
    x_far.start()
    x_y.start()
    x_part.start()

    for cp in small:
        cp.wait()
    lane = lax.broadcasted_iota(jnp.int32, (n_tok, 2 * n_exp), 1)
    low = lane < n_exp
    lane_e = jnp.where(low, lane, lane - n_exp)
    dup = jnp.where(
        lax.broadcasted_iota(jnp.int32, (n_exp, 2 * n_exp), 0)
        == jnp.where(lax.broadcasted_iota(jnp.int32, (n_exp, 2 * n_exp), 1) < n_exp,
                     lax.broadcasted_iota(jnp.int32, (n_exp, 2 * n_exp), 1),
                     lax.broadcasted_iota(jnp.int32, (n_exp, 2 * n_exp), 1) - n_exp),
        1.0, 0.0).astype(jnp.bfloat16)
    cnt = dot(jnp.broadcast_to(cnt_v[...].astype(jnp.float32), (8, n_exp)).astype(jnp.bfloat16), dup)
    limit = jnp.broadcast_to(cnt[0:1, :], (n_tok, 2 * n_exp))
    g = gate_v[...]
    g1 = jnp.minimum(g, BF16_MAX).astype(jnp.bfloat16).astype(jnp.float32)
    g2 = (g - g1).astype(jnp.bfloat16).astype(jnp.float32)
    g3 = (g - g1) - g2
    slot_f = slot_v[...].astype(jnp.float32)
    ids = idx_v[...]
    tab_a = jnp.zeros((n_tok, 2 * n_exp), jnp.float32)
    tab_b = jnp.zeros((n_tok, 2 * n_exp), jnp.float32)
    for j in range(top_k):
        s_j = slot_f[:, j:j + 1]
        kept = (ids[:, j:j + 1] == lane_e) & (s_j >= 0.0) & (s_j < limit)
        tab_a += jnp.where(kept, jnp.where(low, s_j + 1.0, g1[:, j:j + 1]), 0.0)
        tab_b += jnp.where(kept, jnp.where(low, g2[:, j:j + 1], g3[:, j:j + 1]), 0.0)
    ms[ep, :, 0:2 * n_exp] = tab_a.astype(jnp.bfloat16)
    ms[ep, :, 2 * n_exp:4 * n_exp] = tab_b.astype(jnp.bfloat16)
    m_far = remote(ms.at[ep], ms.at[ep], M_FAR, {"ep": far})
    m_part = remote(ms.at[ep], ms.at[ep], M_PART, {"ep": part})
    m_far.start()
    m_part.start()

    def row_of(shape, dim):
        flat = lax.broadcasted_iota(jnp.int32, shape, dim)
        owner = lax.shift_right_logical(flat * 683, 15)
        return flat, owner

    def gather_rows(s):
        flat, owner = row_of((n_rows, 2 * n_exp), 0)
        lanes = lax.broadcasted_iota(jnp.int32, (n_rows, 2 * n_exp), 1)
        sel = jnp.where(lanes == owner + n_local * ep, 1.0, 0.0).astype(jnp.bfloat16)
        at = dot_nt(sel, ms[s, :, 0:2 * n_exp])
        flat, owner = row_of((n_rows, n_tok), 0)
        want = (flat - owner * cap + 1).astype(jnp.float32)
        pick = jnp.where(at == want, 1.0, 0.0).astype(jnp.bfloat16)
        for c, w in chunks(d_model):
            xr[s, :, c:c + w] = dot(pick, xs[s, :, c:c + w]).astype(jnp.bfloat16)

    def build_gates(s):
        lanes = lax.broadcasted_iota(jnp.int32, (2 * n_exp, n_rows), 0)
        _, owner = row_of((2 * n_exp, n_rows), 1)
        sel_lo = jnp.where(lanes == owner + n_local * ep, 1.0, 0.0).astype(jnp.bfloat16)
        sel_hi = jnp.where(lanes == owner + n_local * ep + n_exp, 1.0, 0.0).astype(jnp.bfloat16)
        flat, owner = row_of((n_tok, n_rows), 1)
        want = (flat - owner * cap + 1).astype(jnp.float32)
        a = ms[s, :, 0:2 * n_exp]
        b = ms[s, :, 2 * n_exp:4 * n_exp]
        hit = dot(a, sel_lo) == want
        gm[s, 0] = jnp.where(hit, dot(a, sel_hi), 0.0).astype(jnp.bfloat16)
        gm[s, 1] = jnp.where(hit, dot(b, sel_lo), 0.0).astype(jnp.bfloat16)
        gm[s, 2] = jnp.where(hit, dot(b, sel_hi), 0.0).astype(jnp.bfloat16)

    def hidden(rows, x_val, slot):
        for c, w in chunks(2 * ff):
            hf[0:rows, c:c + w] = dot(x_val, w13b[slot, :, c:c + w])
        for c, w in chunks(ff):
            a = hf[0:rows, c:c + w]
            b = hf[0:rows, ff + c:ff + c + w]
            hb[0:rows, c:c + w] = (jax.nn.silu(a) * b).astype(jnp.bfloat16)

    gather_rows(ep)
    build_gates(ep)
    x_part.wait_recv()
    m_part.wait_recv()
    gather_rows(part)
    build_gates(part)

    x_far.wait_recv()
    x_relay = remote(xs.at[far], xs.at[far], X_RELAY, {"ep": part})
    x_relay.start()
    m_far.wait_recv()
    m_relay = remote(ms.at[far], ms.at[far], M_RELAY, {"ep": part})
    m_relay.start()

    x_y.wait_recv()
    for cp in shared_copies:
        cp.wait()
    hidden(2 * n_tok, jnp.concatenate([xs[ep], xy[...]], axis=0), 0)
    for c, w in chunks(d_model):
        both = dot(hb[0:2 * n_tok, :], w2b[0, :, c:c + w])
        s_own[:, c:c + w] = both[0:n_tok]
        s_send[:, c:c + w] = both[n_tok:2 * n_tok]
    s_copy = remote(s_send, s_recv, S_Y, {"tp": 1 - tp})
    s_copy.start()
    for cp in expert_copies(SLOTS - 1, 0):
        cp.start()

    gather_rows(far)
    build_gates(far)
    x_relay.wait_recv()
    m_relay.wait_recv()
    gather_rows(far_part)
    build_gates(far_part)

    n_src = xs.shape[0]

    def expert_step(e, carry):
        slot = lax.rem(e + 1, SLOTS)
        for cp in expert_copies(e, slot):
            cp.wait()
        rows = pl.ds(pl.multiple_of(e * cap, 16), cap)
        x_val = jnp.concatenate([xr[s, rows, :] for s in range(n_src)], axis=0)
        hidden(n_src * cap, x_val, slot)
        for c, w in chunks(d_model):
            out = dot(hb[0:n_src * cap, :], w2b[slot, :, c:c + w]).astype(jnp.bfloat16)
            for s in range(n_src):
                xr[s, rows, c:c + w] = out[s * cap:(s + 1) * cap]

        @pl.when(e + SLOTS < n_local)
        def _():
            for cp in expert_copies(e + SLOTS, slot):
                cp.start()

        return carry

    lax.fori_loop(0, n_local, expert_step, 0)

    def combine(s, out_ref):
        for c, w in chunks(d_model):
            r = xr[s, :, c:c + w]
            out_ref[:, c:c + w] = dot(gm[s, 0], r) + dot(gm[s, 1], r) + dot(gm[s, 2], r)

    combine(far_part, a_send)
    a_copy = remote(a_send, a_recv, A_PART, {"ep": part})
    a_copy.start()
    combine(far, b_send)
    a_copy.wait_recv()
    b_send[...] += a_recv[...]
    b_copy = remote(b_send, b_recv, B_FAR, {"ep": far})
    b_copy.start()
    combine(part, c_send)
    c_copy = remote(c_send, c_recv, C_PART, {"ep": part})
    c_copy.start()
    for c, w in chunks(d_model):
        r = xr[ep, :, c:c + w]
        own = dot(gm[ep, 0], r) + dot(gm[ep, 1], r) + dot(gm[ep, 2], r)
        s_own[:, c:c + w] += own + xs[ep, :, c:c + w].astype(jnp.float32)
    s_copy.wait_recv()
    c_copy.wait_recv()
    s_own[...] += s_recv[...] + c_recv[...]
    b_copy.wait_recv()
    y_ref[...] = (s_own[...] + b_recv[...]).astype(jnp.bfloat16)

    for cp in (x_far, x_y, x_part, m_far, m_part, x_relay, m_relay, s_copy, a_copy, b_copy, c_copy):
        cp.wait_send()


def solution(mesh):
    row_spec = P(("data", "ep", "tp"), None)
    expert_spec = P("ep", None, None)
    n_src = mesh.shape["ep"]

    def layer_body(tokens, expert_ids, gate_vals, slot_ids, send_counts, shared_w1, shared_w3, shared_w2, expert_w1, expert_w3, expert_w2):
        n_tok, d_model = tokens.shape
        top_k = expert_ids.shape[1]
        n_local, _, ff = expert_w1.shape
        n_exp = n_local * n_src
        cap = capacity_rows(n_tok, top_k, n_exp)
        n_rows = n_local * cap
        block = pltpu.VMEM((n_tok, d_model), jnp.float32)
        return pl.pallas_call(
            functools.partial(kernel, cap, n_local, n_exp),
            out_shape=jax.ShapeDtypeStruct((n_tok, d_model), jnp.bfloat16),
            in_specs=[pl.BlockSpec(memory_space=pl.ANY)] * 11,
            out_specs=pl.BlockSpec(memory_space=pltpu.VMEM),
            scratch_shapes=[
                pltpu.VMEM((n_src, n_tok, d_model), jnp.bfloat16),
                pltpu.VMEM((n_tok, d_model), jnp.bfloat16),
                pltpu.VMEM((n_tok, top_k), jnp.int32),
                pltpu.VMEM((n_tok, top_k), jnp.float32),
                pltpu.VMEM((n_tok, top_k), jnp.int32),
                pltpu.VMEM((1, n_exp), jnp.int32),
                pltpu.VMEM((n_src, n_tok, 4 * n_exp), jnp.bfloat16),
                pltpu.VMEM((SLOTS, d_model, 2 * ff), jnp.bfloat16),
                pltpu.VMEM((SLOTS, ff, d_model), jnp.bfloat16),
                pltpu.VMEM((n_src, n_rows, d_model), jnp.bfloat16),
                pltpu.VMEM((2 * n_tok, 2 * ff), jnp.float32),
                pltpu.VMEM((2 * n_tok, ff), jnp.bfloat16),
                pltpu.VMEM((n_src, 3, n_tok, n_rows), jnp.bfloat16),
            ] + [block] * 9 + [
                pltpu.SemaphoreType.DMA((5,)),
                pltpu.SemaphoreType.DMA((SLOTS, 3)),
                pltpu.SemaphoreType.DMA((N_COPIES,)),
                pltpu.SemaphoreType.DMA((N_COPIES,)),
            ],
            compiler_params=pltpu.CompilerParams(
                collective_id=0, has_side_effects=True, vmem_limit_bytes=67043328),
            name="moe_layer",
        )(tokens, expert_ids, gate_vals, slot_ids, send_counts, shared_w1, shared_w3, shared_w2, expert_w1, expert_w3, expert_w2)

    return jax.shard_map(
        layer_body,
        mesh=mesh,
        in_specs=(row_spec, row_spec, row_spec, row_spec, row_spec, P(None, "tp"), P(None, "tp"), P("tp", None), expert_spec, expert_spec, expert_spec),
        out_specs=row_spec,
        check_vma=False,
    )
```

time: 332 us -> 81.8 us (0.25)
  blocking collectives: 103 us -> 0 us
  Pallas kernels: 0 us -> 75.6 us
  waiting for transfers between devices: 67.5 us -> 0 us
  matrix products: 65.7 us -> 0 us
  local copies, waits for them, and re-layouts: 64.6 us -> 5.97 us
  between operations: 13.6 us -> 0.01 us
  other arithmetic: 11.1 us -> 0 us
  starting transfers between devices: 5.8 us -> 0 us
    all_to_all x1 -> x0, blocking collectives: 92.3 us -> none  [layer_body(): recv_buf = lax.all_to_all(send_buf, 'ep', 0, 2, tiled=True)]
    pallas_call x0 -> x1, Pallas kernels: none -> 75.6 us  [layer_body(): pl.pallas_call(functools.partial(kernel, cap, n_local, n_exp), out_shape=...]
    all_to_all x1 -> x0, waiting for transfers between devices: 67.5 us -> none  [layer_body(): lax.all_to_all(exp_out.reshape(1, n_local, ep_size * capacity, d_model),...]
    dot_general x4 -> x0, matrix products: 65.7 us -> none  [the longest x1 35.3 us: layer_body(): jnp.einsum('erf,efd->erd', exp_hidden, expert_w2, preferred_element_type=...]
    gather x6 -> x0, local copies, waits for them, and re-layouts: 32.8 us -> none  [the longest x1 14.3 us: layer_body(): send_buf = jnp.take(tokens, owner_ids, axis=0, mode='fill', fill_value=0)]
    all_to_all x2 -> x0, local copies, waits for them, and re-layouts: 16.5 us -> none  [the longest x1 9.2 us: layer_body(): lax.all_to_all(exp_out.reshape(1, n_local, ep_size * capacity, d_model),...]
    reshape x3 -> x0, local copies, waits for them, and re-layouts: 11 us -> none  [the longest x1 10.8 us: layer_body(): exp_out.reshape(1, n_local, ep_size * capacity, d_model)]
    all_gather x1 -> x0, blocking collectives: 10.9 us -> none  [layer_body(): gathered = lax.all_gather(tokens, 'tp', axis=0, tiled=True)]
  transfers between devices with their start and end apart: 2 -> 0, of which waited for: 1 -> 0; matrix products, arithmetic and copies ran while one was open for 11% -> 0% of each run, Pallas kernels for 0% -> 0%
where the time goes in v1:
time: 81.8 us; the launch traced here: 81.6 us
  Pallas kernels  75.6 us (92%)
  local copies, waits for them, and re-layouts  5.97 us (7%)
    pallas_call x1, Pallas kernels, layer_body(): pl.pallas_call(functools.partial(kernel, cap, n_local, n_exp), out_shape=...  75.6 us
    unnamed x4, local copies, waits for them, and re-layouts  5.97 us

profile of v1, /device:TPU:0, one launch (start us, length us, event | category | flops | bytes accessed | tf_op | source)
XLA Modules:
  0.0 81.6 jit_solution(11453935040882161880)
XLA Ops:
  0.0 1.4 %copy.12.idx_hbm = s32[128,6]{1,0:T(8,128)} copy(s32[128,6]{0,1:T(8,128)} %param.12) | data formatting | bytes 6144 | tf_op args[1]
  1.4 1.4 %copy.13.gate_hbm = f32[128,6]{1,0:T(8,128)} copy(f32[128,6]{0,1:T(8,128)} %param.13) | data formatting | bytes 6144 | tf_op args[2]
  2.8 1.4 %copy.14.slot_hbm = s32[128,6]{1,0:T(8,128)} copy(s32[128,6]{0,1:T(8,128)} %param.14) | data formatting | bytes 6144 | tf_op args[3]
  4.3 75.6 %moe_layer.1 = bf16[128,1280]{1,0:T(8,128)(2,1)} custom-call(bf16[128,1280]{1,0:T(8,128)(2,1)} %x_hbm.1, s32[128,6]{1,0:T(8,128)} %copy.12.idx_hbm, f32[128,6]{1,0:T(8,128)} %copy.13.gate_hbm, s32[128,6]{1,0:T(8,128)} %copy.14.slot_hbm, s32[1,64]{1,0:T(1,128)} %cnt_hbm.1, bf16[1280,896]{1,0:T(8,128)(2,1)} %ws1_hbm.1, bf16[1280,896]{1,0:T(8,128)(2,1)} %ws3_hbm.1, ...), custom_call_target="tpu_custom_call" | custom-call | tf_op jit(solution)/shard_map/moe_layer/pallas_call | solution.py:269
  79.8 1.7 %copy.16 = bf16[128,1280]{1,0:T(8,128)(2,1)} copy(bf16[128,1280]{1,0:T(8,128)(2,1)} %moe_layer.1) | data formatting | bytes 655360

commit v2 on v1

v2 whole, which is shorter than its diff:
```python
import functools

import jax
import jax.numpy as jnp
from jax import lax
from jax.experimental import pallas as pl
from jax.experimental.pallas import tpu as pltpu
from jax.sharding import PartitionSpec as P

CAP_FACTOR = 4
BF16_MAX = 3.3895313892515355e38
SLOTS = 6

X_PART, X_FAR, X_Y, X_RELAY, M_PART, M_FAR, M_DIAG, S_Y, C_PART = range(9)
N_COPIES = 9


def capacity_rows(n_tok, top_k, n_exp):
    return min(n_tok, ((CAP_FACTOR * n_tok * top_k // n_exp + 7) // 8) * 8)


def chunks(n, step=256):
    return [(i, min(step, n - i)) for i in range(0, n, step)]


def dot(a, b):
    return jnp.dot(a, b, preferred_element_type=jnp.float32)


def dot_nt(a, b):
    return lax.dot_general(a, b, (((1,), (1,)), ((), ())), preferred_element_type=jnp.float32)


def kernel(cap, n_local, split,
           x_hbm, idx_hbm, gate_hbm, slot_hbm, cnt_hbm,
           ws1_hbm, ws3_hbm, ws2_hbm, w1_hbm, w3_hbm, w2_hbm,
           y_ref,
           xs, xy, idx_v, gate_v, slot_v, cnt_v, mt, mr, w13b, w2b, xr, hf, hb, gm_a, gm_b,
           s_own, s_send, s_recv, a_send, a_recv, b_send, b_recv, c_send, c_recv,
           in_sem, w_sem, send_sem, recv_sem, col_send, col_recv):
    n_tok, d_model = x_hbm.shape
    top_k = idx_hbm.shape[0]
    ff = w1_hbm.shape[2]
    n_src = xs.shape[0]
    n_exp = n_src * n_local
    n_rows = n_local * cap
    cols = chunks(d_model)

    ep = lax.axis_index("ep")
    tp = lax.axis_index("tp")
    part = ep + 1 - 2 * lax.rem(ep, 2)
    far = lax.rem(ep + 2, 4)
    far_part = lax.rem(part + 2, 4)

    x_in = pltpu.make_async_copy(x_hbm, xs.at[ep], in_sem.at[0])
    small = [
        pltpu.make_async_copy(idx_hbm, idx_v, in_sem.at[1]),
        pltpu.make_async_copy(gate_hbm, gate_v, in_sem.at[2]),
        pltpu.make_async_copy(slot_hbm, slot_v, in_sem.at[3]),
        pltpu.make_async_copy(cnt_hbm, cnt_v, in_sem.at[4]),
    ]
    x_in.start()
    for cp in small:
        cp.start()

    def weight_copies(r1, r3, r2, slot):
        return [
            pltpu.make_async_copy(r1, w13b.at[slot, :, pl.ds(0, ff)], w_sem.at[slot, 0]),
            pltpu.make_async_copy(r3, w13b.at[slot, :, pl.ds(ff, ff)], w_sem.at[slot, 1]),
            pltpu.make_async_copy(r2, w2b.at[slot], w_sem.at[slot, 2]),
        ]

    def expert_copies(e, slot):
        return weight_copies(w1_hbm.at[e], w3_hbm.at[e], w2_hbm.at[e], slot)

    shared_copies = weight_copies(ws1_hbm, ws3_hbm, ws2_hbm, 0)

    barrier = pltpu.get_barrier_semaphore()
    for dev in ({"ep": part}, {"ep": far}, {"ep": far_part}, {"tp": 1 - tp}):
        pl.semaphore_signal(barrier, inc=1, device_id=dev, device_id_type=pl.DeviceIdType.MESH)
    pl.semaphore_wait(barrier, 4)

    def remote(src, dst, send, recv, dev):
        return pltpu.make_async_remote_copy(
            src_ref=src, dst_ref=dst, send_sem=send, recv_sem=recv,
            device_id=dev, device_id_type=pl.DeviceIdType.MESH)

    def one_copy(src, dst, k, dev):
        return remote(src, dst, send_sem.at[k], recv_sem.at[k], dev)

    x_in.wait()
    x_far = one_copy(xs.at[ep], xs.at[ep], X_FAR, {"ep": far})
    x_y = one_copy(xs.at[ep], xy, X_Y, {"tp": 1 - tp})
    x_part = one_copy(xs.at[ep], xs.at[ep], X_PART, {"ep": part})
    x_far.start()
    x_y.start()
    x_part.start()
    for cp in shared_copies:
        cp.start()

    for cp in small:
        cp.wait()
    eye = (lax.broadcasted_iota(jnp.int32, (n_exp, n_exp), 0)
           == lax.broadcasted_iota(jnp.int32, (n_exp, n_exp), 1))
    diag = jnp.where(eye, jnp.broadcast_to(cnt_v[...], (n_exp, n_exp)).astype(jnp.float32), 0.0)
    limit = dot(diag.astype(jnp.bfloat16), jnp.ones((n_exp, n_tok), jnp.bfloat16))
    g = gate_v[...]
    g1 = jnp.minimum(g, BF16_MAX).astype(jnp.bfloat16).astype(jnp.float32)
    g2 = (g - g1).astype(jnp.bfloat16).astype(jnp.float32)
    g3 = (g - g1) - g2
    slot_f = slot_v[...].astype(jnp.float32)
    ids = idx_v[...]
    row_e = lax.broadcasted_iota(jnp.int32, (n_exp, n_tok), 0)
    tabs = [jnp.zeros((n_exp, n_tok), jnp.float32) for _ in range(4)]
    for j in range(top_k):
        s_j = slot_f[j:j + 1, :]
        kept = (ids[j:j + 1, :] == row_e) & (s_j >= 0.0) & (s_j < limit)
        vals = (s_j + 1.0, g1[j:j + 1, :], g2[j:j + 1, :], g3[j:j + 1, :])
        tabs = [t + jnp.where(kept, v, 0.0) for t, v in zip(tabs, vals)]
    for q in range(n_src):
        for k in range(4):
            mt[q, k * n_local:(k + 1) * n_local, :] = (
                tabs[k][q * n_local:(q + 1) * n_local].astype(jnp.bfloat16))
    m_far = one_copy(mt.at[far], mr.at[ep], M_FAR, {"ep": far})
    m_part = one_copy(mt.at[part], mr.at[ep], M_PART, {"ep": part})
    m_diag = one_copy(mt.at[far_part], mr.at[ep], M_DIAG, {"ep": far_part})
    m_part.start()
    m_far.start()
    m_diag.start()
    mr[ep] = mt[ep]

    for e in range(SLOTS - 1):
        for cp in expert_copies(e, e + 1):
            cp.start()

    def row_of(shape, dim, lo=0):
        flat = lax.broadcasted_iota(jnp.int32, shape, dim) + lo
        owner = lax.shift_right_logical(flat * 683, 15)
        return flat, owner

    def gather_rows(s):
        _, owner = row_of((n_rows, 4 * n_local), 0)
        lanes = lax.broadcasted_iota(jnp.int32, (n_rows, 4 * n_local), 1)
        sel = jnp.where(lanes == owner, 1.0, 0.0).astype(jnp.bfloat16)
        at = dot(sel, mr[s])
        flat, owner = row_of((n_rows, n_tok), 0)
        want = (flat - owner * cap + 1).astype(jnp.float32)
        pick = jnp.where(at == want, 1.0, 0.0).astype(jnp.bfloat16)
        for c, w in cols:
            xr[s, :, c:c + w] = dot(pick, xs[s, :, c:c + w]).astype(jnp.bfloat16)

    def build_gates(s):
        tab = jnp.transpose(mr[s].astype(jnp.float32)).astype(jnp.bfloat16)
        for ref, lo, n in ((gm_a, 0, split * cap), (gm_b, split * cap, n_rows - split * cap)):
            lanes = lax.broadcasted_iota(jnp.int32, (4 * n_local, n), 0)
            _, owner = row_of((4 * n_local, n), 1, lo)
            flat, own_t = row_of((n_tok, n), 1, lo)
            want = (flat - own_t * cap + 1).astype(jnp.float32)
            at = [dot(tab, jnp.where(lanes == owner + k * n_local, 1.0, 0.0).astype(jnp.bfloat16))
                  for k in range(4)]
            hit = at[0] == want
            for k in range(3):
                ref[s, k] = jnp.where(hit, at[k + 1], 0.0).astype(jnp.bfloat16)

    def hidden(rows, x_val, slot):
        for c, w in chunks(2 * ff):
            hf[0:rows, c:c + w] = dot(x_val, w13b[slot, :, c:c + w])
        for c, w in chunks(ff):
            a = hf[0:rows, c:c + w]
            b = hf[0:rows, ff + c:ff + c + w]
            hb[0:rows, c:c + w] = (jax.nn.silu(a) * b).astype(jnp.bfloat16)

    def shared(x_val, out_ref):
        hidden(n_tok, x_val, 0)
        for c, w in cols:
            out_ref[:, c:c + w] = dot(hb[0:n_tok, :], w2b[0, :, c:c + w])

    gather_rows(ep)
    build_gates(ep)
    for cp in shared_copies:
        cp.wait()
    shared(xs[ep], s_own)
    x_part.wait_recv()
    m_part.wait_recv()
    gather_rows(part)
    build_gates(part)

    x_far.wait_recv()
    x_relay = one_copy(xs.at[far], xs.at[far], X_RELAY, {"ep": part})
    x_relay.start()
    x_y.wait_recv()
    shared(xy[...], s_send)
    s_copy = one_copy(s_send, s_recv, S_Y, {"tp": 1 - tp})
    s_copy.start()
    for cp in expert_copies(SLOTS - 1, 0):
        cp.start()

    m_far.wait_recv()
    gather_rows(far)
    build_gates(far)
    x_relay.wait_recv()
    m_diag.wait_recv()
    gather_rows(far_part)
    build_gates(far_part)

    def expert_step(e, carry):
        slot = lax.rem(e + 1, SLOTS)
        for cp in expert_copies(e, slot):
            cp.wait()
        rows = pl.ds(pl.multiple_of(e * cap, 16), cap)
        x_val = jnp.concatenate([xr[s, rows, :] for s in range(n_src)], axis=0)
        hidden(n_src * cap, x_val, slot)
        for c, w in cols:
            out = dot(hb[0:n_src * cap, :], w2b[slot, :, c:c + w]).astype(jnp.bfloat16)
            for s in range(n_src):
                xr[s, rows, c:c + w] = out[s * cap:(s + 1) * cap]

        @pl.when(e + SLOTS < n_local)
        def _():
            for cp in expert_copies(e + SLOTS, slot):
                cp.start()

        return carry

    def combine(gm, s, lo, hi, c, w):
        r = xr[s, lo:hi, c:c + w]
        return dot(gm[s, 0], r) + dot(gm[s, 1], r) + dot(gm[s, 2], r)

    cut = split * cap
    lax.fori_loop(0, split, expert_step, 0)
    for c, w in cols:
        a_send[:, c:c + w] = combine(gm_a, far_part, 0, cut, c, w)
        b_send[:, c:c + w] = combine(gm_a, far, 0, cut, c, w)
        c_send[:, c:c + w] = combine(gm_a, part, 0, cut, c, w)
        s_own[:, c:c + w] += combine(gm_a, ep, 0, cut, c, w) + xs[ep, :, c:c + w].astype(jnp.float32)
    lax.fori_loop(split, n_local, expert_step, 0)

    def col_copy(src, dst, kind, i, dev):
        c, w = cols[i]
        return remote(src.at[:, pl.ds(c, w)], dst.at[:, pl.ds(c, w)],
                      col_send.at[kind, i], col_recv.at[kind, i], dev)

    a_copies = [col_copy(a_send, a_recv, 0, i, {"ep": part}) for i in range(len(cols))]
    b_copies = [col_copy(b_send, b_recv, 1, i, {"ep": far}) for i in range(len(cols))]
    for i, (c, w) in enumerate(cols):
        a_send[:, c:c + w] += combine(gm_b, far_part, cut, n_rows, c, w)
        a_copies[i].start()
    for i, (c, w) in enumerate(cols):
        b_part = b_send[:, c:c + w] + combine(gm_b, far, cut, n_rows, c, w)
        a_copies[i].wait_recv()
        b_send[:, c:c + w] = b_part + a_recv[:, c:c + w]
        b_copies[i].start()
    for c, w in cols:
        c_send[:, c:c + w] += combine(gm_b, part, cut, n_rows, c, w)
    c_copy = one_copy(c_send, c_recv, C_PART, {"ep": part})
    c_copy.start()
    for c, w in cols:
        s_own[:, c:c + w] += combine(gm_b, ep, cut, n_rows, c, w)
    s_copy.wait_recv()
    c_copy.wait_recv()
    s_own[...] += s_recv[...] + c_recv[...]
    for i, (c, w) in enumerate(cols):
        b_copies[i].wait_recv()
        y_ref[:, c:c + w] = (s_own[:, c:c + w] + b_recv[:, c:c + w]).astype(jnp.bfloat16)

    for cp in [x_far, x_y, x_part, m_far, m_part, m_diag, x_relay, s_copy, c_copy] + a_copies + b_copies:
        cp.wait_send()


def solution(mesh):
    row_spec = P(("data", "ep", "tp"), None)
    expert_spec = P("ep", None, None)
    n_src = mesh.shape["ep"]

    def layer_body(tokens, expert_ids, gate_vals, slot_ids, send_counts, shared_w1, shared_w3, shared_w2, expert_w1, expert_w3, expert_w2):
        n_tok, d_model = tokens.shape
        top_k = expert_ids.shape[1]
        n_local, _, ff = expert_w1.shape
        n_exp = n_local * n_src
        cap = capacity_rows(n_tok, top_k, n_exp)
        n_rows = n_local * cap
        split = n_local * 11 // 16
        n_cols = len(chunks(d_model))
        block = pltpu.VMEM((n_tok, d_model), jnp.float32)
        return pl.pallas_call(
            functools.partial(kernel, cap, n_local, split),
            out_shape=pltpu.VMEM((n_tok, d_model), jnp.bfloat16),
            in_specs=[pl.BlockSpec(memory_space=pl.ANY)] * 11,
            out_specs=pl.BlockSpec(memory_space=pltpu.VMEM),
            scratch_shapes=[
                pltpu.VMEM((n_src, n_tok, d_model), jnp.bfloat16),
                pltpu.VMEM((n_tok, d_model), jnp.bfloat16),
                pltpu.VMEM((top_k, n_tok), jnp.int32),
                pltpu.VMEM((top_k, n_tok), jnp.float32),
                pltpu.VMEM((top_k, n_tok), jnp.int32),
                pltpu.VMEM((1, n_exp), jnp.int32),
                pltpu.VMEM((n_src, 4 * n_local, n_tok), jnp.bfloat16),
                pltpu.VMEM((n_src, 4 * n_local, n_tok), jnp.bfloat16),
                pltpu.VMEM((SLOTS, d_model, 2 * ff), jnp.bfloat16),
                pltpu.VMEM((SLOTS, ff, d_model), jnp.bfloat16),
                pltpu.VMEM((n_src, n_rows, d_model), jnp.bfloat16),
                pltpu.VMEM((2 * n_tok, 2 * ff), jnp.float32),
                pltpu.VMEM((2 * n_tok, ff), jnp.bfloat16),
                pltpu.VMEM((n_src, 3, n_tok, split * cap), jnp.bfloat16),
                pltpu.VMEM((n_src, 3, n_tok, n_rows - split * cap), jnp.bfloat16),
            ] + [block] * 9 + [
                pltpu.SemaphoreType.DMA((5,)),
                pltpu.SemaphoreType.DMA((SLOTS, 3)),
                pltpu.SemaphoreType.DMA((N_COPIES,)),
                pltpu.SemaphoreType.DMA((N_COPIES,)),
                pltpu.SemaphoreType.DMA((2, n_cols)),
                pltpu.SemaphoreType.DMA((2, n_cols)),
            ],
            compiler_params=pltpu.CompilerParams(
                collective_id=0, has_side_effects=True, vmem_limit_bytes=66500000),
            name="moe_layer",
        )(tokens, expert_ids.T, gate_vals.T, slot_ids.T, send_counts, shared_w1, shared_w3, shared_w2, expert_w1, expert_w3, expert_w2)

    return jax.shard_map(
        layer_body,
        mesh=mesh,
        in_specs=(row_spec, row_spec, row_spec, row_spec, row_spec, P(None, "tp"), P(None, "tp"), P("tp", None), expert_spec, expert_spec, expert_spec),
        out_specs=row_spec,
        check_vma=False,
    )
```

time: 81.8 us -> 67.9 us (0.83)
  Pallas kernels: 75.6 us -> 67 us
  local copies, waits for them, and re-layouts: 5.97 us -> 0.73 us
    pallas_call x1, Pallas kernels: 75.6 us -> 67 us  [layer_body(): pl.pallas_call(functools.partial(kernel, cap, n_local, split), out_shape=...]
    unnamed x4 -> x1, local copies, waits for them, and re-layouts: 5.97 us -> 0.73 us
where the time goes in v2:
time: 67.9 us; the launch traced here: 67.8 us
  Pallas kernels  67 us (99%)
  local copies, waits for them, and re-layouts  0.73 us (1%)
    pallas_call x1, Pallas kernels, layer_body(): pl.pallas_call(functools.partial(kernel, cap, n_local, split), out_shape=...  67 us

profile of v2, /device:TPU:0, one launch (start us, length us, event | category | flops | bytes accessed | tf_op | source)
XLA Modules:
  0.0 67.8 jit_solution(11894213003132126316)
XLA Ops:
  0.0 67.0 %moe_layer.1 = bf16[128,1280]{1,0:T(8,128)(2,1)S(1)} custom-call(bf16[128,1280]{1,0:T(8,128)(2,1)} %x_hbm.1, s32[6,128]{1,0:T(8,128)} %bitcast.3, f32[6,128]{1,0:T(8,128)} %bitcast.4, s32[6,128]{1,0:T(8,128)} %bitcast.5, s32[1,64]{1,0:T(1,128)} %cnt_hbm.1, bf16[1280,896]{1,0:T(8,128)(2,1)} %ws1_hbm.1, bf16[1280,896]{1,0:T(8,128)(2,1)} %ws3_hbm.1, ...), custom_call_target="tpu_custom_call" | custom-call | tf_op jit(solution)/shard_map/moe_layer/pallas_call | solution.py:285
  67.0 0.7 %copy.13 = bf16[128,1280]{1,0:T(8,128)(2,1)} copy(bf16[128,1280]{1,0:T(8,128)(2,1)S(1)} %moe_layer.1) | data formatting | bytes 655360

commit v3 on v2

v3 whole, which is shorter than its diff:
```python
import functools

import jax
import jax.numpy as jnp
from jax import lax
from jax.experimental import pallas as pl
from jax.experimental.pallas import tpu as pltpu
from jax.sharding import PartitionSpec as P

CAP_FACTOR = 4
BF16_MAX = 3.3895313892515355e38
SLOTS = 6
NEAR = 2

X_PART, X_Y, M_PART, M_FAR, M_DIAG, S_Y, C_PART = range(7)
N_COPIES = 7
COL_X_FAR, COL_X_RELAY, COL_A, COL_B = range(4)
N_COL_KINDS = 4


def capacity_rows(n_tok, top_k, n_exp):
    return min(n_tok, ((CAP_FACTOR * n_tok * top_k // n_exp + 7) // 8) * 8)


def chunks(n, step=256):
    return [(i, min(step, n - i)) for i in range(0, n, step)]


def dot(a, b):
    return jnp.dot(a, b, preferred_element_type=jnp.float32)


def dot_nt(a, b):
    return lax.dot_general(a, b, (((1,), (1,)), ((), ())), preferred_element_type=jnp.float32)


def kernel(cap, n_local,
           x_hbm, idx_hbm, gate_hbm, slot_hbm, cnt_hbm,
           ws1_hbm, ws3_hbm, ws2_hbm, w1_hbm, w3_hbm, w2_hbm,
           y_ref,
           xs, xy, idx_v, gate_v, slot_v, cnt_v, mt, mr, w13b, w2b, xr, hb, pk, gm,
           s_own, s_send, s_recv, a_send, a_recv, b_send, b_recv, c_send, c_recv,
           in_sem, w_sem, send_sem, recv_sem, col_send, col_recv):
    n_tok, d_model = x_hbm.shape
    top_k = idx_hbm.shape[0]
    ff = w1_hbm.shape[2]
    body = ff // 256 * 256
    rest = ff - body
    n_src = xs.shape[0]
    n_exp = n_src * n_local
    n_rows = n_local * cap
    cols = chunks(d_model)

    ep = lax.axis_index("ep")
    tp = lax.axis_index("tp")
    part = ep + 1 - 2 * lax.rem(ep, 2)
    far = lax.rem(ep + 2, 4)
    far_part = lax.rem(part + 2, 4)

    x_in = pltpu.make_async_copy(x_hbm, xs.at[ep], in_sem.at[0])
    small = [
        pltpu.make_async_copy(idx_hbm, idx_v, in_sem.at[1]),
        pltpu.make_async_copy(gate_hbm, gate_v, in_sem.at[2]),
        pltpu.make_async_copy(slot_hbm, slot_v, in_sem.at[3]),
        pltpu.make_async_copy(cnt_hbm, cnt_v, in_sem.at[4]),
    ]
    for cp in small:
        cp.start()
    x_in.start()

    def weight_copies(r1, r3, r2, slot):
        parts = [(r1, 0, 0, body), (r3, 0, body, body),
                 (r1, body, 2 * body, rest), (r3, body, 2 * body + rest, rest)]
        return [
            pltpu.make_async_copy(r.at[:, pl.ds(src, n)], w13b.at[slot, :, pl.ds(dst, n)], w_sem.at[slot, i])
            for i, (r, src, dst, n) in enumerate(parts)
        ] + [pltpu.make_async_copy(r2, w2b.at[slot], w_sem.at[slot, 4])]

    def expert_copies(e, slot):
        return weight_copies(w1_hbm.at[e], w3_hbm.at[e], w2_hbm.at[e], slot)

    def start_all(copies):
        for cp in copies:
            cp.start()

    shared_copies = weight_copies(ws1_hbm, ws3_hbm, ws2_hbm, 0)
    start_all(shared_copies)
    start_all(expert_copies(0, 1))

    barrier = pltpu.get_barrier_semaphore()
    for dev in ({"ep": part}, {"ep": far}, {"ep": far_part}, {"tp": 1 - tp}):
        pl.semaphore_signal(barrier, inc=1, device_id=dev, device_id_type=pl.DeviceIdType.MESH)

    for cp in small:
        cp.wait()
    eye = (lax.broadcasted_iota(jnp.int32, (n_exp, n_exp), 0)
           == lax.broadcasted_iota(jnp.int32, (n_exp, n_exp), 1))
    diag = jnp.where(eye, jnp.broadcast_to(cnt_v[...], (n_exp, n_exp)).astype(jnp.float32), 0.0)
    limit = dot(diag.astype(jnp.bfloat16), jnp.ones((n_exp, n_tok), jnp.bfloat16))
    g = gate_v[...]
    g1 = jnp.minimum(g, BF16_MAX).astype(jnp.bfloat16).astype(jnp.float32)
    g2 = (g - g1).astype(jnp.bfloat16).astype(jnp.float32)
    g3 = (g - g1) - g2
    slot_f = slot_v[...].astype(jnp.float32)
    ids = idx_v[...]
    row_e = lax.broadcasted_iota(jnp.int32, (n_exp, n_tok), 0)
    tabs = [jnp.zeros((n_exp, n_tok), jnp.float32) for _ in range(4)]
    for j in range(top_k):
        s_j = slot_f[j:j + 1, :]
        kept = (ids[j:j + 1, :] == row_e) & (s_j >= 0.0) & (s_j < limit)
        vals = (s_j + 1.0, g1[j:j + 1, :], g2[j:j + 1, :], g3[j:j + 1, :])
        tabs = [t + jnp.where(kept, v, 0.0) for t, v in zip(tabs, vals)]
    for q in range(n_src):
        for k in range(4):
            mt[q, k * n_local:(k + 1) * n_local, :] = (
                tabs[k][q * n_local:(q + 1) * n_local].astype(jnp.bfloat16))
    mr[ep] = mt[ep]

    pl.semaphore_wait(barrier, 4)

    def remote(src, dst, send, recv, dev):
        return pltpu.make_async_remote_copy(
            src_ref=src, dst_ref=dst, send_sem=send, recv_sem=recv,
            device_id=dev, device_id_type=pl.DeviceIdType.MESH)

    def one_copy(src, dst, k, dev):
        return remote(src, dst, send_sem.at[k], recv_sem.at[k], dev)

    def col_copies(src, dst, kind, dev):
        return [remote(src.at[:, pl.ds(c, w)], dst.at[:, pl.ds(c, w)],
                       col_send.at[kind, i], col_recv.at[kind, i], dev)
                for i, (c, w) in enumerate(cols)]

    m_far = one_copy(mt.at[far], mr.at[ep], M_FAR, {"ep": far})
    m_part = one_copy(mt.at[part], mr.at[ep], M_PART, {"ep": part})
    m_diag = one_copy(mt.at[far_part], mr.at[ep], M_DIAG, {"ep": far_part})
    x_far = col_copies(xs.at[ep], xs.at[ep], COL_X_FAR, {"ep": far})
    x_relay = col_copies(xs.at[far], xs.at[far], COL_X_RELAY, {"ep": part})
    x_y = one_copy(xs.at[ep], xy, X_Y, {"tp": 1 - tp})
    x_part = one_copy(xs.at[ep], xs.at[ep], X_PART, {"ep": part})
    m_far.start()
    m_diag.start()
    m_part.start()
    x_in.wait()
    start_all(x_far)
    x_part.start()
    x_y.start()

    for e in range(1, SLOTS - 1):
        start_all(expert_copies(e, e + 1))

    def row_of(shape, dim):
        flat = lax.broadcasted_iota(jnp.int32, shape, dim)
        owner = lax.shift_right_logical(flat * 683, 15)
        return flat, owner

    def build_pick(s, i):
        _, owner = row_of((n_rows, 4 * n_local), 0)
        lanes = lax.broadcasted_iota(jnp.int32, (n_rows, 4 * n_local), 1)
        sel = jnp.where(lanes == owner, 1.0, 0.0).astype(jnp.bfloat16)
        at = dot(sel, mr[s])
        flat, owner = row_of((n_rows, n_tok), 0)
        want = (flat - owner * cap + 1).astype(jnp.float32)
        pk[i] = jnp.where(at == want, 1.0, 0.0).astype(jnp.bfloat16)

    def gather_cols(s, i, c, w):
        xr[s, :, c:c + w] = dot(pk[i], xs[s, :, c:c + w]).astype(jnp.bfloat16)

    def build_gates(s):
        tab = jnp.transpose(mr[s].astype(jnp.float32)).astype(jnp.bfloat16)
        lanes = lax.broadcasted_iota(jnp.int32, (4 * n_local, n_rows), 0)
        _, owner = row_of((4 * n_local, n_rows), 1)
        flat, own_t = row_of((n_tok, n_rows), 1)
        want = (flat - own_t * cap + 1).astype(jnp.float32)
        at = [dot(tab, jnp.where(lanes == owner + k * n_local, 1.0, 0.0).astype(jnp.bfloat16))
              for k in range(4)]
        hit = at[0] == want
        for k in range(3):
            gm[s, k] = jnp.where(hit, at[k + 1], 0.0).astype(jnp.bfloat16)

    def hidden(x_val, slot, h_ref):
        rows = x_val.shape[0]
        for c, w in chunks(body):
            a = dot(x_val, w13b[slot, :, c:c + w])
            b = dot(x_val, w13b[slot, :, body + c:body + c + w])
            h_ref[0:rows, c:c + w] = (jax.nn.silu(a) * b).astype(jnp.bfloat16)
        ab = dot(x_val, w13b[slot, :, 2 * body:2 * ff])
        h_ref[0:rows, body:ff] = (jax.nn.silu(ab[:, 0:rest]) * ab[:, rest:2 * rest]).astype(jnp.bfloat16)

    def shared(x_val, out_ref):
        hidden(x_val, 0, hb.at[0])
        for c, w in cols:
            out_ref[:, c:c + w] = dot(hb[0, 0:n_tok, :], w2b[0, :, c:c + w])

    def wait_expert(e, slot):
        for cp in expert_copies(e, slot):
            cp.wait()

    def expert_rows(e, slot, sources, i):
        rows = pl.ds(pl.multiple_of(e * cap, 16), cap)
        n = len(sources) * cap
        hidden(jnp.concatenate([xr[s, rows, :] for s in sources], axis=0), slot, hb.at[i])
        for c, w in cols:
            out = dot(hb[i, 0:n, :], w2b[slot, :, c:c + w]).astype(jnp.bfloat16)
            for k, s in enumerate(sources):
                xr[s, rows, c:c + w] = out[k * cap:(k + 1) * cap]

    build_pick(ep, 0)
    for c, w in cols:
        gather_cols(ep, 0, c, w)
    m_part.wait_recv()
    build_pick(part, 1)
    x_part.wait_recv()
    for c, w in cols:
        gather_cols(part, 1, c, w)
    for cp in shared_copies:
        cp.wait()
    shared(xs[ep], s_own)
    m_far.wait_recv()
    build_pick(far, 0)
    build_gates(far)
    m_diag.wait_recv()
    build_pick(far_part, 1)
    build_gates(far_part)
    for e in range(NEAR):
        wait_expert(e, e + 1)
    for e in range(NEAR):
        expert_rows(e, e + 1, (ep, part), e % 2)

    for i, (c, w) in enumerate(cols):
        x_far[i].wait_recv()
        x_relay[i].start()
        gather_cols(far, 0, c, w)
    x_y.wait_recv()
    shared(xy[...], s_send)
    s_copy = one_copy(s_send, s_recv, S_Y, {"tp": 1 - tp})
    s_copy.start()
    start_all(expert_copies(SLOTS - 1, 0))
    for i, (c, w) in enumerate(cols):
        x_relay[i].wait_recv()
        gather_cols(far_part, 1, c, w)
    for e in range(NEAR):
        expert_rows(e, e + 1, (far, far_part), e % 2)
    for e in range(NEAR):
        start_all(expert_copies(e + SLOTS, e + 1))

    def pair_step(p, carry):
        both = [(2 * p + i, lax.rem(2 * p + i + 1, SLOTS)) for i in range(2)]
        for e, slot in both:
            wait_expert(e, slot)
        for i, (e, slot) in enumerate(both):
            expert_rows(e, slot, range(n_src), i)

        @pl.when(2 * p + SLOTS < n_local)
        def _():
            for e, slot in both:
                start_all(expert_copies(e + SLOTS, slot))

        return carry

    lax.fori_loop(NEAR // 2, n_local // 2, pair_step, 0)

    def combine(s, c, w):
        r = xr[s, :, c:c + w]
        return dot(gm[s, 0], r) + dot(gm[s, 1], r) + dot(gm[s, 2], r)

    a_copies = col_copies(a_send, a_recv, COL_A, {"ep": part})
    b_copies = col_copies(b_send, b_recv, COL_B, {"ep": far})
    for i, (c, w) in enumerate(cols):
        a_send[:, c:c + w] = combine(far_part, c, w)
        a_copies[i].start()
    for i, (c, w) in enumerate(cols):
        b_part = combine(far, c, w)
        a_copies[i].wait_recv()
        b_send[:, c:c + w] = b_part + a_recv[:, c:c + w]
        b_copies[i].start()
    build_gates(part)
    for c, w in cols:
        c_send[:, c:c + w] = combine(part, c, w)
    c_copy = one_copy(c_send, c_recv, C_PART, {"ep": part})
    c_copy.start()
    build_gates(ep)
    for c, w in cols:
        s_own[:, c:c + w] += combine(ep, c, w) + xs[ep, :, c:c + w].astype(jnp.float32)
    s_copy.wait_recv()
    c_copy.wait_recv()
    s_own[...] += s_recv[...] + c_recv[...]
    for i, (c, w) in enumerate(cols):
        b_copies[i].wait_recv()
        y_ref[:, c:c + w] = (s_own[:, c:c + w] + b_recv[:, c:c + w]).astype(jnp.bfloat16)

    for cp in [x_y, x_part, m_far, m_part, m_diag, s_copy, c_copy] + x_far + x_relay + a_copies + b_copies:
        cp.wait_send()


def solution(mesh):
    row_spec = P(("data", "ep", "tp"), None)
    expert_spec = P("ep", None, None)
    n_src = mesh.shape["ep"]

    def layer_body(tokens, expert_ids, gate_vals, slot_ids, send_counts, shared_w1, shared_w3, shared_w2, expert_w1, expert_w3, expert_w2):
        n_tok, d_model = tokens.shape
        top_k = expert_ids.shape[1]
        n_local, _, ff = expert_w1.shape
        n_exp = n_local * n_src
        cap = capacity_rows(n_tok, top_k, n_exp)
        n_rows = n_local * cap
        n_cols = len(chunks(d_model))
        block = pltpu.VMEM((n_tok, d_model), jnp.float32)
        return pl.pallas_call(
            functools.partial(kernel, cap, n_local),
            out_shape=pltpu.VMEM((n_tok, d_model), jnp.bfloat16),
            in_specs=[pl.BlockSpec(memory_space=pl.ANY)] * 11,
            out_specs=pl.BlockSpec(memory_space=pltpu.VMEM),
            scratch_shapes=[
                pltpu.VMEM((n_src, n_tok, d_model), jnp.bfloat16),
                pltpu.VMEM((n_tok, d_model), jnp.bfloat16),
                pltpu.VMEM((top_k, n_tok), jnp.int32),
                pltpu.VMEM((top_k, n_tok), jnp.float32),
                pltpu.VMEM((top_k, n_tok), jnp.int32),
                pltpu.VMEM((1, n_exp), jnp.int32),
                pltpu.VMEM((n_src, 4 * n_local, n_tok), jnp.bfloat16),
                pltpu.VMEM((n_src, 4 * n_local, n_tok), jnp.bfloat16),
                pltpu.VMEM((SLOTS, d_model, 2 * ff), jnp.bfloat16),
                pltpu.VMEM((SLOTS, ff, d_model), jnp.bfloat16),
                pltpu.VMEM((n_src, n_rows, d_model), jnp.bfloat16),
                pltpu.VMEM((2, n_src * cap, ff), jnp.bfloat16),
                pltpu.VMEM((2, n_rows, n_tok), jnp.bfloat16),
                pltpu.VMEM((n_src, 3, n_tok, n_rows), jnp.bfloat16),
            ] + [block] * 9 + [
                pltpu.SemaphoreType.DMA((5,)),
                pltpu.SemaphoreType.DMA((SLOTS, 5)),
                pltpu.SemaphoreType.DMA((N_COPIES,)),
                pltpu.SemaphoreType.DMA((N_COPIES,)),
                pltpu.SemaphoreType.DMA((N_COL_KINDS, n_cols)),
                pltpu.SemaphoreType.DMA((N_COL_KINDS, n_cols)),
            ],
            compiler_params=pltpu.CompilerParams(
                collective_id=0, has_side_effects=True, vmem_limit_bytes=66500000),
            name="moe_layer",
        )(tokens, expert_ids.T, gate_vals.T, slot_ids.T, send_counts, shared_w1, shared_w3, shared_w2, expert_w1, expert_w3, expert_w2)

    return jax.shard_map(
        layer_body,
        mesh=mesh,
        in_specs=(row_spec, row_spec, row_spec, row_spec, row_spec, P(None, "tp"), P(None, "tp"), P("tp", None), expert_spec, expert_spec, expert_spec),
        out_specs=row_spec,
        check_vma=False,
    )
```

time: 67.9 us -> 66.5 us (0.979)
  Pallas kernels: 67 us -> 65.7 us
    pallas_call x1, Pallas kernels: 67 us -> 65.7 us  [layer_body(): pl.pallas_call(functools.partial(kernel, cap, n_local), out_shape=pltpu.V...]
where the time goes in v3:
time: 66.5 us; the launch traced here: 66.4 us
  Pallas kernels  65.7 us (99%)
  local copies, waits for them, and re-layouts  0.73 us (1%)
    pallas_call x1, Pallas kernels, layer_body(): pl.pallas_call(functools.partial(kernel, cap, n_local), out_shape=pltpu.V...  65.7 us

profile of v3, /device:TPU:0, one launch (start us, length us, event | category | flops | bytes accessed | tf_op | source)
XLA Modules:
  0.0 66.4 jit_solution(4802250716236826574)
XLA Ops:
  0.0 65.7 %moe_layer.1 = bf16[128,1280]{1,0:T(8,128)(2,1)S(1)} custom-call(bf16[128,1280]{1,0:T(8,128)(2,1)} %x_hbm.1, s32[6,128]{1,0:T(8,128)} %bitcast.3, f32[6,128]{1,0:T(8,128)} %bitcast.4, s32[6,128]{1,0:T(8,128)} %bitcast.5, s32[1,64]{1,0:T(1,128)} %cnt_hbm.1, bf16[1280,896]{1,0:T(8,128)(2,1)} %ws1_hbm.1, bf16[1280,896]{1,0:T(8,128)(2,1)} %ws3_hbm.1, ...), custom_call_target="tpu_custom_call" | custom-call | tf_op jit(solution)/shard_map/moe_layer/pallas_call | solution.py:310
  65.7 0.7 %copy.13 = bf16[128,1280]{1,0:T(8,128)(2,1)} copy(bf16[128,1280]{1,0:T(8,128)(2,1)S(1)} %moe_layer.1) | data formatting | bytes 655360

commit v4 on v3

--- a/solution.py
+++ b/solution.py
@@ -38,9 +38,9 @@
            x_hbm, idx_hbm, gate_hbm, slot_hbm, cnt_hbm,
            ws1_hbm, ws3_hbm, ws2_hbm, w1_hbm, w3_hbm, w2_hbm,
            y_ref,
-           xs, xy, idx_v, gate_v, slot_v, cnt_v, mt, mr, w13b, w2b, xr, hb, pk, gm,
+           xs, xy, idx_v, gate_v, slot_v, cnt_v, mt, mr,
            s_own, s_send, s_recv, a_send, a_recv, b_send, b_recv, c_send, c_recv,
-           in_sem, w_sem, send_sem, recv_sem, col_send, col_recv):
+           in_sem, w_sem, send_sem, recv_sem, col_send, col_recv, w13b, w2b, xr, hb, pk, gm):
     n_tok, d_model = x_hbm.shape
     top_k = idx_hbm.shape[0]
     ff = w1_hbm.shape[2]
@@ -307,8 +307,20 @@
         n_rows = n_local * cap
         n_cols = len(chunks(d_model))
         block = pltpu.VMEM((n_tok, d_model), jnp.float32)
+        local = [
+                pltpu.VMEM((SLOTS, d_model, 2 * ff), jnp.bfloat16),
+                pltpu.VMEM((SLOTS, ff, d_model), jnp.bfloat16),
+                pltpu.VMEM((n_src, n_rows, d_model), jnp.bfloat16),
+                pltpu.VMEM((2, n_src * cap, ff), jnp.bfloat16),
+                pltpu.VMEM((2, n_rows, n_tok), jnp.bfloat16),
+                pltpu.VMEM((n_src, 3, n_tok, n_rows), jnp.bfloat16),
+        ]
+
+        def body(*refs):
+            pl.run_scoped(functools.partial(kernel, cap, n_local, *refs), *local)
+
         return pl.pallas_call(
-            functools.partial(kernel, cap, n_local),
+            body,
             out_shape=pltpu.VMEM((n_tok, d_model), jnp.bfloat16),
             in_specs=[pl.BlockSpec(memory_space=pl.ANY)] * 11,
             out_specs=pl.BlockSpec(memory_space=pltpu.VMEM),
@@ -321,12 +333,6 @@
                 pltpu.VMEM((1, n_exp), jnp.int32),
                 pltpu.VMEM((n_src, 4 * n_local, n_tok), jnp.bfloat16),
                 pltpu.VMEM((n_src, 4 * n_local, n_tok), jnp.bfloat16),
-                pltpu.VMEM((SLOTS, d_model, 2 * ff), jnp.bfloat16),
-                pltpu.VMEM((SLOTS, ff, d_model), jnp.bfloat16),
-                pltpu.VMEM((n_src, n_rows, d_model), jnp.bfloat16),
-                pltpu.VMEM((2, n_src * cap, ff), jnp.bfloat16),
-                pltpu.VMEM((2, n_rows, n_tok), jnp.bfloat16),
-                pltpu.VMEM((n_src, 3, n_tok, n_rows), jnp.bfloat16),
             ] + [block] * 9 + [
                 pltpu.SemaphoreType.DMA((5,)),
                 pltpu.SemaphoreType.DMA((SLOTS, 5)),

time: 66.5 us -> 64.5 us (0.970)
  Pallas kernels: 65.7 us -> 63.6 us
    pallas_call x1, Pallas kernels: 65.7 us -> 63.6 us  [layer_body(): pl.pallas_call(body, out_shape=pltpu.VMEM((n_tok, d_model), jnp.bfloat16)...]
where the time goes in v4:
time: 64.5 us; the launch traced here: 64.4 us
  Pallas kernels  63.6 us (99%)
  local copies, waits for them, and re-layouts  0.73 us (1%)
    pallas_call x1, Pallas kernels, layer_body(): pl.pallas_call(body, out_shape=pltpu.VMEM((n_tok, d_model), jnp.bfloat16)...  63.6 us

profile of v4, /device:TPU:0, one launch (start us, length us, event | category | flops | bytes accessed | tf_op | source)
XLA Modules:
  0.0 64.4 jit_solution(5059549352063175802)
XLA Ops:
  0.0 63.6 %moe_layer.1 = bf16[128,1280]{1,0:T(8,128)(2,1)S(1)} custom-call(bf16[128,1280]{1,0:T(8,128)(2,1)} %refs_0_.1, s32[6,128]{1,0:T(8,128)} %bitcast.3, f32[6,128]{1,0:T(8,128)} %bitcast.4, s32[6,128]{1,0:T(8,128)} %bitcast.5, s32[1,64]{1,0:T(1,128)} %refs_4_.1, bf16[1280,896]{1,0:T(8,128)(2,1)} %refs_5_.1, bf16[1280,896]{1,0:T(8,128)(2,1)} %refs_6_.1, ...), custom_call_target="tpu_custom_call" | custom-call | tf_op jit(solution)/shard_map/moe_layer/pallas_call | solution.py:322
  63.7 0.7 %copy.13 = bf16[128,1280]{1,0:T(8,128)(2,1)} copy(bf16[128,1280]{1,0:T(8,128)(2,1)S(1)} %moe_layer.1) | data formatting | bytes 655360

commit v5 on v4

--- a/solution.py
+++ b/solution.py
@@ -11,6 +11,7 @@
 BF16_MAX = 3.3895313892515355e38
 SLOTS = 6
 NEAR = 2
+LAST = 6
 
 X_PART, X_Y, M_PART, M_FAR, M_DIAG, S_Y, C_PART = range(7)
 N_COPIES = 7
@@ -39,8 +40,8 @@
            ws1_hbm, ws3_hbm, ws2_hbm, w1_hbm, w3_hbm, w2_hbm,
            y_ref,
            xs, xy, idx_v, gate_v, slot_v, cnt_v, mt, mr,
-           s_own, s_send, s_recv, a_send, a_recv, b_send, b_recv, c_send, c_recv,
-           in_sem, w_sem, send_sem, recv_sem, col_send, col_recv, w13b, w2b, xr, hb, pk, gm):
+           s_own, s_send, s_recv, a_send, a_recv, b_recv,
+           in_sem, w_sem, send_sem, recv_sem, col_send, col_recv, free_sem, w13b, w2b, xr, hb, pk, gm):
     n_tok, d_model = x_hbm.shape
     top_k = idx_hbm.shape[0]
     ff = w1_hbm.shape[2]
@@ -69,12 +70,11 @@
     x_in.start()
 
     def weight_copies(r1, r3, r2, slot):
-        parts = [(r1, 0, 0, body), (r3, 0, body, body),
-                 (r1, body, 2 * body, rest), (r3, body, 2 * body + rest, rest)]
         return [
-            pltpu.make_async_copy(r.at[:, pl.ds(src, n)], w13b.at[slot, :, pl.ds(dst, n)], w_sem.at[slot, i])
-            for i, (r, src, dst, n) in enumerate(parts)
-        ] + [pltpu.make_async_copy(r2, w2b.at[slot], w_sem.at[slot, 4])]
+            pltpu.make_async_copy(r1, w13b.at[slot, :, pl.ds(0, ff)], w_sem.at[slot, 0]),
+            pltpu.make_async_copy(r3, w13b.at[slot, :, pl.ds(ff, ff)], w_sem.at[slot, 1]),
+            pltpu.make_async_copy(r2, w2b.at[slot], w_sem.at[slot, 2]),
+        ]
 
     def expert_copies(e, slot):
         return weight_copies(w1_hbm.at[e], w3_hbm.at[e], w2_hbm.at[e], slot)
@@ -166,7 +166,7 @@
     def gather_cols(s, i, c, w):
         xr[s, :, c:c + w] = dot(pk[i], xs[s, :, c:c + w]).astype(jnp.bfloat16)
 
-    def build_gates(s):
+    def build_gates(s, i):
         tab = jnp.transpose(mr[s].astype(jnp.float32)).astype(jnp.bfloat16)
         lanes = lax.broadcasted_iota(jnp.int32, (4 * n_local, n_rows), 0)
         _, owner = row_of((4 * n_local, n_rows), 1)
@@ -176,15 +176,15 @@
               for k in range(4)]
         hit = at[0] == want
         for k in range(3):
-            gm[s, k] = jnp.where(hit, at[k + 1], 0.0).astype(jnp.bfloat16)
+            gm[i, k] = jnp.where(hit, at[k + 1], 0.0).astype(jnp.bfloat16)
 
     def hidden(x_val, slot, h_ref):
         rows = x_val.shape[0]
         for c, w in chunks(body):
             a = dot(x_val, w13b[slot, :, c:c + w])
-            b = dot(x_val, w13b[slot, :, body + c:body + c + w])
+            b = dot(x_val, w13b[slot, :, ff + c:ff + c + w])
             h_ref[0:rows, c:c + w] = (jax.nn.silu(a) * b).astype(jnp.bfloat16)
-        ab = dot(x_val, w13b[slot, :, 2 * body:2 * ff])
+        ab = dot(x_val, jnp.concatenate([w13b[slot, :, body:ff], w13b[slot, :, ff + body:2 * ff]], axis=1))
         h_ref[0:rows, body:ff] = (jax.nn.silu(ab[:, 0:rest]) * ab[:, rest:2 * rest]).astype(jnp.bfloat16)
 
     def shared(x_val, out_ref):
@@ -196,10 +196,16 @@
         for cp in expert_copies(e, slot):
             cp.wait()
 
+    def expert_slice(e):
+        return pl.ds(pl.multiple_of(e * cap, 16), cap)
+
+    def take_rows(e, sources):
+        return jnp.concatenate([xr[s, expert_slice(e), :] for s in sources], axis=0)
+
     def expert_rows(e, slot, sources, i):
-        rows = pl.ds(pl.multiple_of(e * cap, 16), cap)
+        rows = expert_slice(e)
         n = len(sources) * cap
-        hidden(jnp.concatenate([xr[s, rows, :] for s in sources], axis=0), slot, hb.at[i])
+        hidden(take_rows(e, sources), slot, hb.at[i])
         for c, w in cols:
             out = dot(hb[i, 0:n, :], w2b[slot, :, c:c + w]).astype(jnp.bfloat16)
             for k, s in enumerate(sources):
@@ -218,10 +224,10 @@
     shared(xs[ep], s_own)
     m_far.wait_recv()
     build_pick(far, 0)
-    build_gates(far)
+    build_gates(far, 0)
     m_diag.wait_recv()
     build_pick(far_part, 1)
-    build_gates(far_part)
+    build_gates(far_part, 1)
     for e in range(NEAR):
         wait_expert(e, e + 1)
     for e in range(NEAR):
@@ -251,45 +257,83 @@
         for i, (e, slot) in enumerate(both):
             expert_rows(e, slot, range(n_src), i)
 
-        @pl.when(2 * p + SLOTS < n_local)
-        def _():
-            for e, slot in both:
+        for e, slot in both:
+            @pl.when(e + SLOTS < n_local)
+            def _():
                 start_all(expert_copies(e + SLOTS, slot))
 
         return carry
 
-    lax.fori_loop(NEAR // 2, n_local // 2, pair_step, 0)
-
-    def combine(s, c, w):
+    late = n_local - LAST
+    lax.fori_loop(NEAR // 2, late // 2, pair_step, 0)
+
+    def late_hidden(t, carry):
+        both = [(late + 2 * t + i, lax.rem(late + 2 * t + i + 1, SLOTS)) for i in range(2)]
+        for e, slot in both:
+            for cp in expert_copies(e, slot)[0:2]:
+                cp.wait()
+        for i, (e, slot) in enumerate(both):
+            hidden(take_rows(e, (far, far_part)), slot, hb.at[t, pl.ds(2 * i * cap, 2 * cap)])
+        return carry
+
+    lax.fori_loop(0, LAST // 2, late_hidden, 0)
+    for e in range(late, n_local):
+        expert_copies(e, (e + 1) % SLOTS)[2].wait()
+
+    def combine(s, i, c, w):
         r = xr[s, :, c:c + w]
-        return dot(gm[s, 0], r) + dot(gm[s, 1], r) + dot(gm[s, 2], r)
+        return dot(gm[i, 0], r) + dot(gm[i, 1], r) + dot(gm[i, 2], r)
 
     a_copies = col_copies(a_send, a_recv, COL_A, {"ep": part})
-    b_copies = col_copies(b_send, b_recv, COL_B, {"ep": far})
+    b_copies = col_copies(s_send, b_recv, COL_B, {"ep": far})
+    s_copy.wait_send()
+
+    def finish_b(i):
+        c, w = cols[i]
+        a_copies[i].wait_recv()
+        s_send[:, c:c + w] += a_recv[:, c:c + w]
+        b_copies[i].start()
+
     for i, (c, w) in enumerate(cols):
-        a_send[:, c:c + w] = combine(far_part, c, w)
+        for k, e in enumerate(range(late, n_local)):
+            h = hb[k // 2, 2 * (k % 2) * cap:2 * (k % 2 + 1) * cap, :]
+            out = dot(h, w2b[(e + 1) % SLOTS, :, c:c + w]).astype(jnp.bfloat16)
+            xr[far, e * cap:(e + 1) * cap, c:c + w] = out[0:cap]
+            xr[far_part, e * cap:(e + 1) * cap, c:c + w] = out[cap:2 * cap]
+        a_send[:, c:c + w] = combine(far_part, 1, c, w)
         a_copies[i].start()
-    for i, (c, w) in enumerate(cols):
-        b_part = combine(far, c, w)
-        a_copies[i].wait_recv()
-        b_send[:, c:c + w] = b_part + a_recv[:, c:c + w]
-        b_copies[i].start()
-    build_gates(part)
+        s_send[:, c:c + w] = combine(far, 0, c, w)
+        if i > 0:
+            finish_b(i - 1)
+    build_gates(part, 0)
+    finish_b(len(cols) - 1)
+    pl.semaphore_signal(free_sem, inc=1, device_id={"ep": part}, device_id_type=pl.DeviceIdType.MESH)
+    build_gates(ep, 1)
+
+    def late_near(t, carry):
+        for i in range(2):
+            e = late + 2 * t + i
+            expert_rows(e, lax.rem(e + 1, SLOTS), (ep, part), i)
+        return carry
+
+    lax.fori_loop(0, LAST // 2, late_near, 0)
+    for cp in a_copies:
+        cp.wait_send()
     for c, w in cols:
-        c_send[:, c:c + w] = combine(part, c, w)
-    c_copy = one_copy(c_send, c_recv, C_PART, {"ep": part})
+        a_send[:, c:c + w] = combine(part, 0, c, w)
+    c_copy = one_copy(a_send, a_recv, C_PART, {"ep": part})
+    pl.semaphore_wait(free_sem, 1)
     c_copy.start()
-    build_gates(ep)
     for c, w in cols:
-        s_own[:, c:c + w] += combine(ep, c, w) + xs[ep, :, c:c + w].astype(jnp.float32)
+        s_own[:, c:c + w] += combine(ep, 1, c, w) + xs[ep, :, c:c + w].astype(jnp.float32)
     s_copy.wait_recv()
     c_copy.wait_recv()
-    s_own[...] += s_recv[...] + c_recv[...]
+    s_own[...] += s_recv[...] + a_recv[...]
     for i, (c, w) in enumerate(cols):
         b_copies[i].wait_recv()
         y_ref[:, c:c + w] = (s_own[:, c:c + w] + b_recv[:, c:c + w]).astype(jnp.bfloat16)
 
-    for cp in [x_y, x_part, m_far, m_part, m_diag, s_copy, c_copy] + x_far + x_relay + a_copies + b_copies:
+    for cp in [x_y, x_part, m_far, m_part, m_diag, c_copy] + x_far + x_relay + b_copies:
         cp.wait_send()
 
 
@@ -311,9 +355,9 @@
                 pltpu.VMEM((SLOTS, d_model, 2 * ff), jnp.bfloat16),
                 pltpu.VMEM((SLOTS, ff, d_model), jnp.bfloat16),
                 pltpu.VMEM((n_src, n_rows, d_model), jnp.bfloat16),
-                pltpu.VMEM((2, n_src * cap, ff), jnp.bfloat16),
+                pltpu.VMEM((LAST // 2, n_src * cap, ff), jnp.bfloat16),
                 pltpu.VMEM((2, n_rows, n_tok), jnp.bfloat16),
-                pltpu.VMEM((n_src, 3, n_tok, n_rows), jnp.bfloat16),
+                pltpu.VMEM((2, 3, n_tok, n_rows), jnp.bfloat16),
         ]
 
         def body(*refs):
@@ -333,13 +377,14 @@
                 pltpu.VMEM((1, n_exp), jnp.int32),
                 pltpu.VMEM((n_src, 4 * n_local, n_tok), jnp.bfloat16),
                 pltpu.VMEM((n_src, 4 * n_local, n_tok), jnp.bfloat16),
-            ] + [block] * 9 + [
+            ] + [block] * 6 + [
                 pltpu.SemaphoreType.DMA((5,)),
-                pltpu.SemaphoreType.DMA((SLOTS, 5)),
+                pltpu.SemaphoreType.DMA((SLOTS, 3)),
                 pltpu.SemaphoreType.DMA((N_COPIES,)),
                 pltpu.SemaphoreType.DMA((N_COPIES,)),
                 pltpu.SemaphoreType.DMA((N_COL_KINDS, n_cols)),
                 pltpu.SemaphoreType.DMA((N_COL_KINDS, n_cols)),
+                pltpu.SemaphoreType.REGULAR,
             ],
             compiler_params=pltpu.CompilerParams(
                 collective_id=0, has_side_effects=True, vmem_limit_bytes=66500000),

time: 64.5 us -> 61.1 us (0.947)
  Pallas kernels: 63.6 us -> 60.2 us
    pallas_call x1, Pallas kernels: 63.6 us -> 60.2 us  [layer_body(): pl.pallas_call(body, out_shape=pltpu.VMEM((n_tok, d_model), jnp.bfloat16)...]
where the time goes in v5:
time: 61.1 us; the launch traced here: 61 us
  Pallas kernels  60.2 us (99%)
  local copies, waits for them, and re-layouts  0.73 us (1%)
    pallas_call x1, Pallas kernels, layer_body(): pl.pallas_call(body, out_shape=pltpu.VMEM((n_tok, d_model), jnp.bfloat16)...  60.2 us

profile of v5, /device:TPU:0, one launch (start us, length us, event | category | flops | bytes accessed | tf_op | source)
XLA Modules:
  0.0 61.0 jit_solution(12993098500210531108)
XLA Ops:
  0.0 60.2 %moe_layer.1 = bf16[128,1280]{1,0:T(8,128)(2,1)S(1)} custom-call(bf16[128,1280]{1,0:T(8,128)(2,1)} %refs_0_.1, s32[6,128]{1,0:T(8,128)} %bitcast.3, f32[6,128]{1,0:T(8,128)} %bitcast.4, s32[6,128]{1,0:T(8,128)} %bitcast.5, s32[1,64]{1,0:T(1,128)} %refs_4_.1, bf16[1280,896]{1,0:T(8,128)(2,1)} %refs_5_.1, bf16[1280,896]{1,0:T(8,128)(2,1)} %refs_6_.1, ...), custom_call_target="tpu_custom_call" | custom-call | tf_op jit(solution)/shard_map/moe_layer/pallas_call | solution.py:366
  60.2 0.7 %copy.13 = bf16[128,1280]{1,0:T(8,128)(2,1)} copy(bf16[128,1280]{1,0:T(8,128)(2,1)S(1)} %moe_layer.1) | data formatting | bytes 655360

commit v6 on v5

--- a/solution.py
+++ b/solution.py
@@ -9,7 +9,8 @@
 
 CAP_FACTOR = 4
 BF16_MAX = 3.3895313892515355e38
-SLOTS = 6
+RING_A = 7
+RING_B = 6
 NEAR = 2
 LAST = 6
 
@@ -41,7 +42,7 @@
            y_ref,
            xs, xy, idx_v, gate_v, slot_v, cnt_v, mt, mr,
            s_own, s_send, s_recv, a_send, a_recv, b_recv,
-           in_sem, w_sem, send_sem, recv_sem, col_send, col_recv, free_sem, w13b, w2b, xr, hb, pk, gm):
+           in_sem, a_sem, b_sem, send_sem, recv_sem, col_send, col_recv, free_sem, w13b, w2b, xr, hb, pk, gm):
     n_tok, d_model = x_hbm.shape
     top_k = idx_hbm.shape[0]
     ff = w1_hbm.shape[2]
@@ -69,23 +70,30 @@
         cp.start()
     x_in.start()
 
-    def weight_copies(r1, r3, r2, slot):
+    def copies_a(r1, r3, step):
+        at = lax.rem(step, RING_A)
         return [
-            pltpu.make_async_copy(r1, w13b.at[slot, :, pl.ds(0, ff)], w_sem.at[slot, 0]),
-            pltpu.make_async_copy(r3, w13b.at[slot, :, pl.ds(ff, ff)], w_sem.at[slot, 1]),
-            pltpu.make_async_copy(r2, w2b.at[slot], w_sem.at[slot, 2]),
+            pltpu.make_async_copy(r1, w13b.at[at, :, pl.ds(0, ff)], a_sem.at[at, 0]),
+            pltpu.make_async_copy(r3, w13b.at[at, :, pl.ds(ff, ff)], a_sem.at[at, 1]),
         ]
 
-    def expert_copies(e, slot):
-        return weight_copies(w1_hbm.at[e], w3_hbm.at[e], w2_hbm.at[e], slot)
+    def copies_b(r2, step):
+        at = lax.rem(step, RING_B)
+        return [pltpu.make_async_copy(r2, w2b.at[at], b_sem.at[at])]
+
+    def expert_a(e):
+        return copies_a(w1_hbm.at[e], w3_hbm.at[e], e + 1)
+
+    def expert_b(e):
+        return copies_b(w2_hbm.at[e], e + 1)
 
     def start_all(copies):
         for cp in copies:
             cp.start()
 
-    shared_copies = weight_copies(ws1_hbm, ws3_hbm, ws2_hbm, 0)
+    shared_copies = copies_a(ws1_hbm, ws3_hbm, 0) + copies_b(ws2_hbm, 0)
     start_all(shared_copies)
-    start_all(expert_copies(0, 1))
+    start_all(expert_a(0) + expert_b(0))
 
     barrier = pltpu.get_barrier_semaphore()
     for dev in ({"ep": part}, {"ep": far}, {"ep": far_part}, {"tp": 1 - tp}):
@@ -146,8 +154,10 @@
     x_part.start()
     x_y.start()
 
-    for e in range(1, SLOTS - 1):
-        start_all(expert_copies(e, e + 1))
+    for e in range(1, RING_A - 1):
+        start_all(expert_a(e))
+        if e < RING_B - 1:
+            start_all(expert_b(e))
 
     def row_of(shape, dim):
         flat = lax.broadcasted_iota(jnp.int32, shape, dim)
@@ -178,8 +188,9 @@
         for k in range(3):
             gm[i, k] = jnp.where(hit, at[k + 1], 0.0).astype(jnp.bfloat16)
 
-    def hidden(x_val, slot, h_ref):
+    def hidden(x_val, step, h_ref):
         rows = x_val.shape[0]
+        slot = lax.rem(step, RING_A)
         for c, w in chunks(body):
             a = dot(x_val, w13b[slot, :, c:c + w])
             b = dot(x_val, w13b[slot, :, ff + c:ff + c + w])
@@ -192,9 +203,15 @@
         for c, w in cols:
             out_ref[:, c:c + w] = dot(hb[0, 0:n_tok, :], w2b[0, :, c:c + w])
 
-    def wait_expert(e, slot):
-        for cp in expert_copies(e, slot):
+    def wait_expert(e):
+        for cp in expert_a(e) + expert_b(e):
             cp.wait()
+
+    def refill(e):
+        for copies, ring in ((expert_a, RING_A), (expert_b, RING_B)):
+            @pl.when(e + ring < n_local)
+            def _():
+                start_all(copies(e + ring))
 
     def expert_slice(e):
         return pl.ds(pl.multiple_of(e * cap, 16), cap)
@@ -202,12 +219,12 @@
     def take_rows(e, sources):
         return jnp.concatenate([xr[s, expert_slice(e), :] for s in sources], axis=0)
 
-    def expert_rows(e, slot, sources, i):
+    def expert_rows(e, sources, i):
         rows = expert_slice(e)
         n = len(sources) * cap
-        hidden(take_rows(e, sources), slot, hb.at[i])
+        hidden(take_rows(e, sources), e + 1, hb.at[i])
         for c, w in cols:
-            out = dot(hb[i, 0:n, :], w2b[slot, :, c:c + w]).astype(jnp.bfloat16)
+            out = dot(hb[i, 0:n, :], w2b[lax.rem(e + 1, RING_B), :, c:c + w]).astype(jnp.bfloat16)
             for k, s in enumerate(sources):
                 xr[s, rows, c:c + w] = out[k * cap:(k + 1) * cap]
 
@@ -228,10 +245,12 @@
     m_diag.wait_recv()
     build_pick(far_part, 1)
     build_gates(far_part, 1)
+    build_gates(part, 2)
+    build_gates(ep, 3)
     for e in range(NEAR):
-        wait_expert(e, e + 1)
+        wait_expert(e)
     for e in range(NEAR):
-        expert_rows(e, e + 1, (ep, part), e % 2)
+        expert_rows(e, (ep, part), e % 2)
 
     for i, (c, w) in enumerate(cols):
         x_far[i].wait_recv()
@@ -241,26 +260,22 @@
     shared(xy[...], s_send)
     s_copy = one_copy(s_send, s_recv, S_Y, {"tp": 1 - tp})
     s_copy.start()
-    start_all(expert_copies(SLOTS - 1, 0))
+    start_all(expert_b(RING_B - 1) + expert_a(RING_A - 1))
     for i, (c, w) in enumerate(cols):
         x_relay[i].wait_recv()
         gather_cols(far_part, 1, c, w)
     for e in range(NEAR):
-        expert_rows(e, e + 1, (far, far_part), e % 2)
-    for e in range(NEAR):
-        start_all(expert_copies(e + SLOTS, e + 1))
+        expert_rows(e, (far, far_part), e % 2)
+        start_all(expert_b(e + RING_B) + expert_a(e + RING_A))
 
     def pair_step(p, carry):
-        both = [(2 * p + i, lax.rem(2 * p + i + 1, SLOTS)) for i in range(2)]
-        for e, slot in both:
-            wait_expert(e, slot)
-        for i, (e, slot) in enumerate(both):
-            expert_rows(e, slot, range(n_src), i)
-
-        for e, slot in both:
-            @pl.when(e + SLOTS < n_local)
-            def _():
-                start_all(expert_copies(e + SLOTS, slot))
+        both = [2 * p + i for i in range(2)]
+        for e in both:
+            wait_expert(e)
+        for i, e in enumerate(both):
+            expert_rows(e, range(n_src), i)
+        for e in both:
+            refill(e)
 
         return carry
 
@@ -268,17 +283,18 @@
     lax.fori_loop(NEAR // 2, late // 2, pair_step, 0)
 
     def late_hidden(t, carry):
-        both = [(late + 2 * t + i, lax.rem(late + 2 * t + i + 1, SLOTS)) for i in range(2)]
-        for e, slot in both:
-            for cp in expert_copies(e, slot)[0:2]:
+        both = [late + 2 * t + i for i in range(2)]
+        for e in both:
+            for cp in expert_a(e):
                 cp.wait()
-        for i, (e, slot) in enumerate(both):
-            hidden(take_rows(e, (far, far_part)), slot, hb.at[t, pl.ds(2 * i * cap, 2 * cap)])
+        for i, e in enumerate(both):
+            hidden(take_rows(e, (far, far_part)), e + 1, hb.at[t, pl.ds(2 * i * cap, 2 * cap)])
         return carry
 
     lax.fori_loop(0, LAST // 2, late_hidden, 0)
     for e in range(late, n_local):
-        expert_copies(e, (e + 1) % SLOTS)[2].wait()
+        for cp in expert_b(e):
+            cp.wait()
 
     def combine(s, i, c, w):
         r = xr[s, :, c:c + w]
@@ -297,7 +313,7 @@
     for i, (c, w) in enumerate(cols):
         for k, e in enumerate(range(late, n_local)):
             h = hb[k // 2, 2 * (k % 2) * cap:2 * (k % 2 + 1) * cap, :]
-            out = dot(h, w2b[(e + 1) % SLOTS, :, c:c + w]).astype(jnp.bfloat16)
+            out = dot(h, w2b[(e + 1) % RING_B, :, c:c + w]).astype(jnp.bfloat16)
             xr[far, e * cap:(e + 1) * cap, c:c + w] = out[0:cap]
             xr[far_part, e * cap:(e + 1) * cap, c:c + w] = out[cap:2 * cap]
         a_send[:, c:c + w] = combine(far_part, 1, c, w)
@@ -305,27 +321,25 @@
         s_send[:, c:c + w] = combine(far, 0, c, w)
         if i > 0:
             finish_b(i - 1)
-    build_gates(part, 0)
     finish_b(len(cols) - 1)
     pl.semaphore_signal(free_sem, inc=1, device_id={"ep": part}, device_id_type=pl.DeviceIdType.MESH)
-    build_gates(ep, 1)
 
     def late_near(t, carry):
         for i in range(2):
             e = late + 2 * t + i
-            expert_rows(e, lax.rem(e + 1, SLOTS), (ep, part), i)
+            expert_rows(e, (ep, part), i)
         return carry
 
     lax.fori_loop(0, LAST // 2, late_near, 0)
     for cp in a_copies:
         cp.wait_send()
     for c, w in cols:
-        a_send[:, c:c + w] = combine(part, 0, c, w)
+        a_send[:, c:c + w] = combine(part, 2, c, w)
     c_copy = one_copy(a_send, a_recv, C_PART, {"ep": part})
     pl.semaphore_wait(free_sem, 1)
     c_copy.start()
     for c, w in cols:
-        s_own[:, c:c + w] += combine(ep, 1, c, w) + xs[ep, :, c:c + w].astype(jnp.float32)
+        s_own[:, c:c + w] += combine(ep, 3, c, w) + xs[ep, :, c:c + w].astype(jnp.float32)
     s_copy.wait_recv()
     c_copy.wait_recv()
     s_own[...] += s_recv[...] + a_recv[...]
@@ -352,12 +366,12 @@
         n_cols = len(chunks(d_model))
         block = pltpu.VMEM((n_tok, d_model), jnp.float32)
         local = [
-                pltpu.VMEM((SLOTS, d_model, 2 * ff), jnp.bfloat16),
-                pltpu.VMEM((SLOTS, ff, d_model), jnp.bfloat16),
+                pltpu.VMEM((RING_A, d_model, 2 * ff), jnp.bfloat16),
+                pltpu.VMEM((RING_B, ff, d_model), jnp.bfloat16),
                 pltpu.VMEM((n_src, n_rows, d_model), jnp.bfloat16),
                 pltpu.VMEM((LAST // 2, n_src * cap, ff), jnp.bfloat16),
                 pltpu.VMEM((2, n_rows, n_tok), jnp.bfloat16),
-                pltpu.VMEM((2, 3, n_tok, n_rows), jnp.bfloat16),
+                pltpu.VMEM((4, 3, n_tok, n_rows), jnp.bfloat16),
         ]
 
         def body(*refs):
@@ -379,7 +393,8 @@
                 pltpu.VMEM((n_src, 4 * n_local, n_tok), jnp.bfloat16),
             ] + [block] * 6 + [
                 pltpu.SemaphoreType.DMA((5,)),
-                pltpu.SemaphoreType.DMA((SLOTS, 3)),
+                pltpu.SemaphoreType.DMA((RING_A, 2)),
+                pltpu.SemaphoreType.DMA((RING_B,)),
                 pltpu.SemaphoreType.DMA((N_COPIES,)),
                 pltpu.SemaphoreType.DMA((N_COPIES,)),
                 pltpu.SemaphoreType.DMA((N_COL_KINDS, n_cols)),

time: 61.1 us -> 59 us (0.966)
  Pallas kernels: 60.2 us -> 58.2 us
    pallas_call x1, Pallas kernels: 60.2 us -> 58.2 us  [layer_body(): pl.pallas_call(body, out_shape=pltpu.VMEM((n_tok, d_model), jnp.bfloat16)...]
where the time goes in v6:
time: 59 us; the launch traced here: 58.9 us
  Pallas kernels  58.2 us (99%)
  local copies, waits for them, and re-layouts  0.73 us (1%)
    pallas_call x1, Pallas kernels, layer_body(): pl.pallas_call(body, out_shape=pltpu.VMEM((n_tok, d_model), jnp.bfloat16)...  58.2 us

profile of v6, /device:TPU:0, one launch (start us, length us, event | category | flops | bytes accessed | tf_op | source)
XLA Modules:
  0.0 58.9 jit_solution(11464854949641965263)
XLA Ops:
  0.0 58.2 %moe_layer.1 = bf16[128,1280]{1,0:T(8,128)(2,1)S(1)} custom-call(bf16[128,1280]{1,0:T(8,128)(2,1)} %refs_0_.1, s32[6,128]{1,0:T(8,128)} %bitcast.3, f32[6,128]{1,0:T(8,128)} %bitcast.4, s32[6,128]{1,0:T(8,128)} %bitcast.5, s32[1,64]{1,0:T(1,128)} %refs_4_.1, bf16[1280,896]{1,0:T(8,128)(2,1)} %refs_5_.1, bf16[1280,896]{1,0:T(8,128)(2,1)} %refs_6_.1, ...), custom_call_target="tpu_custom_call" | custom-call | tf_op jit(solution)/shard_map/moe_layer/pallas_call | solution.py:380
  58.2 0.7 %copy.13 = bf16[128,1280]{1,0:T(8,128)(2,1)} copy(bf16[128,1280]{1,0:T(8,128)(2,1)S(1)} %moe_layer.1) | data formatting | bytes 655360
